TPU v7x, 1024 devices: a whole 8x8x8 slice. The times are simulated.
1024 devices in a mesh: gx: 16 (over x, core), gy: 8 (over z), gz: 8 (over y).
Axes of the slice: x: 8, y: 8, z: 8, core: 2. Of those that a mesh axis runs over, the one named last changes fastest.
Arguments:
- divergence: float32 [256, 128, 1024], P('gx', 'gy', 'gz'), may hold values from -6 to 6
- damping: float32 [256, 128, 1024], P('gx', 'gy', 'gz'), may hold values from 5e-06 to 0.004
Outputs:
- potential: float32 [256, 128, 1024], P('gx', 'gy', 'gz')
All inputs are finite; a program needn't handle non-finite values.
Results may differ from a plain program's by a relative error of at most 0.0001.
Values sent between devices are 32-bit elements; how exact they have to be, the bound alone decides.
A program may use at most 64 MiB of HBM per device.

v0:
```python
import math

import jax
import jax.numpy as jnp
from jax import lax
from jax.sharding import PartitionSpec as P

LEVELS = 4
PRE = 2
POST = 2


relax_weight = 2.0 / 3.0


def with_halo(block, sides, width):
    for axis, dim in sides:
        count = lax.axis_size(axis)
        forward = [(i, i + 1) for i in range(count - 1)]
        backward = [(target, source) for source, target in forward]
        low = lax.ppermute(
            lax.slice_in_dim(block, block.shape[dim] - width, None, axis=dim), axis, forward
        )
        high = lax.ppermute(lax.slice_in_dim(block, 0, width, axis=dim), axis, backward)
        block = jnp.concatenate([low, block, high], axis=dim)
    return block


def laid_out(parts, dim):
    parts = jnp.moveaxis(parts, 0, dim)
    shape = parts.shape
    return parts.reshape(*shape[:dim], shape[dim] * shape[dim + 1], *shape[dim + 2 :])


def sent_to_all(shard, axis):
    length = lax.axis_size(axis)
    return lax.all_to_all(
        jnp.broadcast_to(shard[None], (length, *shard.shape)), axis, 0, 0, tiled=True
    )


def gather_directly(shard, axis, dim):
    return laid_out(sent_to_all(shard, axis), dim)


def neighbour_sum(padded):
    total = padded[2:, 1:-1, 1:-1] + padded[:-2, 1:-1, 1:-1]
    total = total + padded[1:-1, 2:, 1:-1] + padded[1:-1, :-2, 1:-1]
    total = total + padded[1:-1, 1:-1, 2:] + padded[1:-1, 1:-1, :-2]
    return total


def apply_level(values, padded, damping_level, coupling):
    return (6.0 * values - neighbour_sum(padded)) * coupling + damping_level * values


def relaxed_sweep(values, padded, source, damping_level, coupling):
    diagonal = 6.0 * coupling + damping_level
    return (
        values
        + relax_weight * (source - apply_level(values, padded, damping_level, coupling)) / diagonal
    )


def coarsen(values, block_x, block_y, block_z):
    size_x, size_y, size_z = values.shape
    shaped = values.reshape(
        size_x // block_x, block_x, size_y // block_y, block_y, size_z // block_z, block_z
    )
    return shaped.mean(axis=(1, 3, 5))


def refine(values, block_x, block_y, block_z):
    return jnp.repeat(jnp.repeat(jnp.repeat(values, block_x, 0), block_y, 1), block_z, 2)


def sine_table(points, dtype):
    indices = jnp.arange(points, dtype=dtype) + 1.0
    return math.sqrt(2.0 / (points + 1)) * jnp.sin(
        math.pi * indices[:, None] * indices[None, :] / (points + 1)
    )


def eigen_values(points, spacing, dtype):
    indices = jnp.arange(points, dtype=dtype) + 1.0
    return (2.0 - 2.0 * jnp.cos(math.pi * indices / (points + 1))) / (spacing * spacing)


def coarse_solve(source, damping_mean, spacing_x, spacing_y, spacing_z):
    size_x, size_y, size_z = source.shape
    dtype = source.dtype
    table_x = sine_table(size_x, dtype)
    table_y = sine_table(size_y, dtype)
    table_z = sine_table(size_z, dtype)
    spectrum = jnp.einsum(
        "ai,bj,ck,ijk->abc", table_x, table_y, table_z, source, precision=lax.Precision.HIGHEST
    )
    denominator = (
        eigen_values(size_x, spacing_x, dtype)[:, None, None]
        + eigen_values(size_y, spacing_y, dtype)[None, :, None]
        + eigen_values(size_z, spacing_z, dtype)[None, None, :]
        + damping_mean
    )
    spectrum = spectrum / denominator
    return jnp.einsum(
        "ia,jb,kc,abc->ijk", table_x, table_y, table_z, spectrum, precision=lax.Precision.HIGHEST
    )


def trimmed(block_data, margin):
    return block_data[
        margin : block_data.shape[0] - margin,
        margin : block_data.shape[1] - margin,
        margin : block_data.shape[2] - margin,
    ]


def inside_mask(block_shape, margin, dtype):
    along_x = (
        lax.axis_index("gx") * block_shape[0]
        + jnp.arange(block_shape[0] + 2 * margin, dtype=jnp.int32)
        - margin
    )
    along_y = (
        lax.axis_index("gy") * block_shape[1]
        + jnp.arange(block_shape[1] + 2 * margin, dtype=jnp.int32)
        - margin
    )
    along_z = (
        lax.axis_index("gz") * block_shape[2]
        + jnp.arange(block_shape[2] + 2 * margin, dtype=jnp.int32)
        - margin
    )
    inside_x = (along_x >= 0) & (along_x < block_shape[0] * lax.axis_size("gx"))
    inside_y = (along_y >= 0) & (along_y < block_shape[1] * lax.axis_size("gy"))
    inside_z = (along_z >= 0) & (along_z < block_shape[2] * lax.axis_size("gz"))
    joined = inside_x[:, None, None] & inside_y[None, :, None] & inside_z[None, None, :]
    return joined.astype(dtype)


def deep_presmooth(source, damping_level, coupling):
    both_ext = with_halo(jnp.stack([source, damping_level]), (("gx", 1), ("gy", 2), ("gz", 3)), PRE)
    source_ext = both_ext[0]
    damping_ext = both_ext[1]
    inside = inside_mask(source.shape, PRE, source.dtype)
    values = relax_weight * source_ext / (6.0 * coupling + damping_ext)
    values = relaxed_sweep(
        trimmed(values, 1), values, trimmed(source_ext, 1), trimmed(damping_ext, 1), coupling
    ) * trimmed(inside, 1)
    core = trimmed(values, 1)
    remainder = source - apply_level(core, values, damping_level, coupling)
    return (core, remainder)


def deep_postsmooth(values, source, damping_level, coupling):
    stacked = with_halo(
        jnp.stack([values, source, damping_level]), (("gx", 1), ("gy", 2), ("gz", 3)), POST
    )
    current = stacked[0]
    source_ext = stacked[1]
    damping_ext = stacked[2]
    inside = inside_mask(values.shape, POST, values.dtype)
    for sweep_index in range(POST):
        margin = sweep_index + 1
        current = relaxed_sweep(
            trimmed(current, 1),
            current,
            trimmed(source_ext, margin),
            trimmed(damping_ext, margin),
            coupling,
        ) * trimmed(inside, margin)
    return current


def local(divergence, damping):
    cells_x, cells_y, cells_z = divergence.shape
    dampings = [damping]
    for level_index in range(1, LEVELS):
        dampings.append(coarsen(dampings[-1], 2, 2, 2))
    sources = []
    smoothed = []
    source = divergence
    for level_index in range(LEVELS):
        coupling = 0.25**level_index
        values, remainder = deep_presmooth(source, dampings[level_index], coupling)
        sources.append(source)
        smoothed.append(values)
        if level_index + 1 < LEVELS:
            source = coarsen(remainder, 2, 2, 2)
    payload = jnp.stack([jnp.mean(remainder), jnp.mean(dampings[-1])]).reshape(1, 2)
    plane_table = gather_directly(payload, ("gy", "gz"), 0)
    coarse_table = gather_directly(plane_table, "gx", 0)
    count_x = lax.axis_size("gx")
    count_y = lax.axis_size("gy")
    count_z = lax.axis_size("gz")
    coarse_table = coarse_table.reshape(count_x, count_y, count_z, 2)
    solution = coarse_solve(
        coarse_table[:, :, :, 0], jnp.mean(coarse_table[:, :, :, 1]), cells_x, cells_y, cells_z
    )
    own_index = (lax.axis_index("gx") * count_y + lax.axis_index("gy")) * count_z + lax.axis_index(
        "gz"
    )
    correction = lax.dynamic_slice_in_dim(solution.reshape(-1), own_index, 1).reshape(1, 1, 1)
    for level_index in reversed(range(LEVELS)):
        coupling = 0.25**level_index
        values = smoothed[level_index] + correction
        values = deep_postsmooth(values, sources[level_index], dampings[level_index], coupling)
        if level_index > 0:
            correction = refine(values, 2, 2, 2)
    return values


def solution(mesh):
    in_specs = (P("gx", "gy", "gz"), P("gx", "gy", "gz"))
    out_specs = P("gx", "gy", "gz")
    return jax.shard_map(local, mesh=mesh, in_specs=in_specs, out_specs=out_specs, check_vma=False)
```

profile of v0, /device:TPU:1, one launch (start us, length us, event | category | flops | bytes accessed | tf_op | source)
XLA Modules:
  0.0 320.6 jit_solution(5703092736354740242)
XLA Ops:
  0.8 4.5 %collective-permute-start = (f32[2,2,16,128]{3,2,1,0:T(8,128)S(1)}, f32[2,2,16,128]{3,2,1,0:T(8,128)S(1)}, u32[]{:S(2)}, u32[]{:S(2)}) collective-permute-start(f32[2,2,16,128]{3,2,1,0:T(8,128)S(1)} %get-tuple-element.27), channel_id=1, source_target_pairs={{0,64},{64,128},{128,192},{192,256},{256,320},{320,384},{384,448},... | collective-permute-start | bytes 98312 | tf_op jit(solution)/shard_map/ppermute | solution.py:21
  5.3 12.8 %collective-permute-start.1 = (f32[2,2,16,128]{3,2,1,0:T(8,128)S(1)}, f32[2,2,16,128]{3,2,1,0:T(8,128)S(1)}, u32[]{:S(2)}, u32[]{:S(2)}) collective-permute-start(f32[2,2,16,128]{3,2,1,0:T(8,128)S(1)} %get-tuple-element.28), channel_id=1, source_target_pairs={{64,0},{128,64},{192,128},{256,192},{320,256},{384,320},{448,384},... | collective-permute-start | bytes 98312 | tf_op jit(solution)/shard_map/ppermute | solution.py:24
  18.1 10.5 %reshape.414 = f32[8,2,8,2,64,2]{5,4,3,2,1,0:T(8,128)} reshape(f32[16,16,128]{2,1,0:T(8,128)} %param.3) | data formatting | bytes 262144 | tf_op jit(solution)/shard_map/reshape | solution.py:67
  28.6 4.1 %reduce_sum.82 = f32[8,8,64]{2,1,0:T(8,128)S(1)} reduce(f32[8,2,8,2,64,2]{5,4,3,2,1,0:T(8,128)} %reshape.414, f32[]{:T(128)} %constant.50.clone.1), dimensions={1,3,5}, to_apply=%region_1.0 | reduce | flops 28672 | bytes 147460 | tf_op jit(solution)/shard_map/reduce_sum | solution.py:70
  43.0 7.3 %collective-permute-done.4 = f32[2,20,20,2]{3,0,2,1:T(2,128)S(1)} collective-permute-done((f32[2,20,20,2]{3,0,2,1:T(2,128)S(1)}, f32[2,20,20,2]{3,0,2,1:T(2,128)S(1)}, u32[]{:S(2)}, u32[]{:S(2)}) %collective-permute-start.4) | collective-permute-done | bytes 6432 | tf_op jit(solution)/shard_map/ppermute | solution.py:21
  50.3 3.9 %collective-permute-done.5 = f32[2,20,20,2]{3,0,2,1:T(2,128)S(1)} collective-permute-done((f32[2,20,20,2]{3,0,2,1:T(2,128)S(1)}, f32[2,20,20,2]{3,0,2,1:T(2,128)S(1)}, u32[]{:S(2)}, u32[]{:S(2)}) %collective-permute-start.5) | collective-permute-done | bytes 6432 | tf_op jit(solution)/shard_map/ppermute | solution.py:24
  57.8 9.8 %reshape.413 = f32[8,2,8,2,64,2]{5,4,3,2,1,0:T(8,128)} reshape(f32[16,16,128]{2,1,0:T(8,128)S(1)} %fusion.22) | data formatting | bytes 262144 | tf_op jit(solution)/shard_map/reshape | solution.py:67
  67.6 4.0 %reduce_sum.81 = f32[8,8,64]{2,1,0:T(8,128)S(1)} reduce(f32[8,2,8,2,64,2]{5,4,3,2,1,0:T(8,128)} %reshape.413, f32[]{:T(128)} %constant.50.clone.1), dimensions={1,3,5}, to_apply=%region_0.0 | reduce | flops 28672 | bytes 147460 | tf_op jit(solution)/shard_map/reduce_sum | solution.py:70
  83.2 5.9 %collective-permute-done.9 = f32[2,12,2,64]{3,2,1,0:T(2,128)S(1)} collective-permute-done((f32[2,12,2,64]{3,2,1,0:T(2,128)S(1)}, f32[2,12,2,64]{3,2,1,0:T(2,128)S(1)}, u32[]{:S(2)}, u32[]{:S(2)}) %collective-permute-start.9) | collective-permute-done | bytes 12320 | tf_op jit(solution)/shard_map/ppermute | solution.py:24
  96.0 4.9 %collective-permute-done.11 = f32[2,12,12,2]{3,0,2,1:T(2,128)S(1)} collective-permute-done((f32[2,12,12,2]{3,0,2,1:T(2,128)S(1)}, f32[2,12,12,2]{3,0,2,1:T(2,128)S(1)}, u32[]{:S(2)}, u32[]{:S(2)}) %collective-permute-start.11) | collective-permute-done | bytes 2336 | tf_op jit(solution)/shard_map/ppermute | solution.py:24
  104.4 4.1 %collective-permute-start.12 = (f32[2,2,4,32]{3,2,1,0:T(4,128)S(1)}, f32[2,2,4,32]{3,2,1,0:T(4,128)S(1)}, u32[]{:S(2)}, u32[]{:S(2)}) collective-permute-start(f32[2,2,4,32]{3,2,1,0:T(4,128)S(1)} %get-tuple-element.69), channel_id=1, source_target_pairs={{0,64},{64,128},{128,192},{192,256},{256,320},{320,384},{384,448},... | collective-permute-start | bytes 6152 | tf_op jit(solution)/shard_map/ppermute | solution.py:21
  113.4 4.6 %collective-permute-start.14 = (f32[2,8,2,32]{3,2,1,0:T(2,128)S(1)}, f32[2,8,2,32]{3,2,1,0:T(2,128)S(1)}, u32[]{:S(2)}, u32[]{:S(2)}) collective-permute-start(f32[2,8,2,32]{3,2,1,0:T(2,128)S(1)} %get-tuple-element.63), channel_id=1, source_target_pairs={{0,8},{8,16},{16,24},{24,32},{32,40},{40,48},{48,56},{1,9},{9,17},... | collective-permute-start | bytes 12296 | tf_op jit(solution)/shard_map/ppermute | solution.py:21
  122.7 4.6 %collective-permute-start.16 = (f32[2,8,8,2]{3,2,1,0:T(8,128)S(1)}, f32[2,8,8,2]{3,2,1,0:T(8,128)S(1)}, u32[]{:S(2)}, u32[]{:S(2)}) collective-permute-start(f32[2,8,8,2]{3,2,1,0:T(8,128)S(1)} %get-tuple-element.53), channel_id=1, source_target_pairs={{0,1},{1,2},{2,3},{3,4},{4,5},{5,6},{6,7},{8,9},{9,10},{10,11},{11... | collective-permute-start | bytes 3080 | tf_op jit(solution)/shard_map/ppermute | solution.py:21
  129.2 3.9 %collective-permute-done.17 = f32[2,8,8,2]{3,2,1,0:T(8,128)S(1)} collective-permute-done((f32[2,8,8,2]{3,2,1,0:T(8,128)S(1)}, f32[2,8,8,2]{3,2,1,0:T(8,128)S(1)}, u32[]{:S(2)}, u32[]{:S(2)}) %collective-permute-start.17) | collective-permute-done | bytes 1056 | tf_op jit(solution)/shard_map/ppermute | solution.py:24
  134.0 4.9 %collective-permute-start.18 = (f32[2,2,2,16]{3,2,1,0:T(2,128)S(1)}, f32[2,2,2,16]{3,2,1,0:T(2,128)S(1)}, u32[]{:S(2)}, u32[]{:S(2)}) collective-permute-start(f32[2,2,2,16]{3,2,1,0:T(2,128)S(1)} %pad_maximum_fusion.43), channel_id=1, source_target_pairs={{0,64},{64,128},{128,192},{192,256},{256,320},{320,384},{384,448},... | collective-permute-start | bytes 1544 | tf_op jit(solution)/shard_map/ppermute | solution.py:21
  143.8 4.6 %collective-permute-start.20 = (f32[2,6,2,16]{3,2,1,0:T(2,128)S(1)}, f32[2,6,2,16]{3,2,1,0:T(2,128)S(1)}, u32[]{:S(2)}, u32[]{:S(2)}) collective-permute-start(f32[2,6,2,16]{3,2,1,0:T(2,128)S(1)} %pad_maximum_fusion.40), channel_id=1, source_target_pairs={{0,8},{8,16},{16,24},{24,32},{32,40},{40,48},{48,56},{1,9},{9,17},... | collective-permute-start | bytes 4616 | tf_op jit(solution)/shard_map/ppermute | solution.py:21
  165.2 9.7 %all-to-all-start = ((f32[64,1,2]{2,1,0:T(1,128)}), f32[64,1,2]{2,1,0:T(1,128)S(1)}, u32[]{:S(2)}, u32[]{:S(2)}) async-start(f32[64,1,2]{2,1,0:T(1,128)} %broadcast_in_dim.24), calls=%async_computation | async-start | bytes 65536 | tf_op jit(solution)/shard_map/all_to_all | solution.py:37
  174.9 10.8 %all-to-all-done = f32[64,1,2]{2,1,0:T(1,128)S(1)} async-done(((f32[64,1,2]{2,1,0:T(1,128)}), f32[64,1,2]{2,1,0:T(1,128)S(1)}, u32[]{:S(2)}, u32[]{:S(2)}) %all-to-all-start) | async-done | bytes 544 | tf_op jit(solution)/shard_map/all_to_all | solution.py:37
  186.4 10.0 %all-to-all-start.1 = ((f32[16,1,128]{2,1,0:T(1,128)}), f32[16,1,128]{2,1,0:T(1,128)S(1)}, u32[]{:S(2)}, u32[]{:S(2)}) async-start(f32[16,1,128]{2,1,0:T(1,128)} %reshape.429), calls=%async_computation.1 | async-start | bytes 16384 | tf_op jit(solution)/shard_map/all_to_all | solution.py:37
  196.5 6.9 %all-to-all-done.1 = f32[16,1,128]{2,1,0:T(1,128)S(1)} async-done(((f32[16,1,128]{2,1,0:T(1,128)}), f32[16,1,128]{2,1,0:T(1,128)S(1)}, u32[]{:S(2)}, u32[]{:S(2)}) %all-to-all-start.1) | async-done | bytes 8224 | tf_op jit(solution)/shard_map/all_to_all | solution.py:37
  233.6 4.0 %collective-permute-start.30 = (f32[3,2,4,32]{3,2,1,0:T(4,128)S(1)}, f32[3,2,4,32]{3,2,1,0:T(4,128)S(1)}, u32[]{:S(2)}, u32[]{:S(2)}) collective-permute-start(f32[3,2,4,32]{3,2,1,0:T(4,128)S(1)} %get-tuple-element.67), channel_id=1, source_target_pairs={{0,64},{64,128},{128,192},{192,256},{256,320},{320,384},{384,448},... | collective-permute-start | bytes 9224 | tf_op jit(solution)/shard_map/ppermute | solution.py:21
  254.5 3.9 %collective-permute-done.35 = f32[3,8,8,2]{3,2,1,0:T(8,128)S(1)} collective-permute-done((f32[3,8,8,2]{3,2,1,0:T(8,128)S(1)}, f32[3,8,8,2]{3,2,1,0:T(8,128)S(1)}, u32[]{:S(2)}, u32[]{:S(2)}) %collective-permute-start.35) | collective-permute-done | bytes 1568 | tf_op jit(solution)/shard_map/ppermute | solution.py:24
  278.8 5.3 %collective-permute-done.40 = f32[3,12,12,2]{3,2,1,0:T(8,128)S(1)} collective-permute-done((f32[3,12,12,2]{3,2,1,0:T(8,128)S(1)}, f32[3,12,12,2]{3,2,1,0:T(8,128)S(1)}, u32[]{:S(2)}, u32[]{:S(2)}) %collective-permute-start.40) | collective-permute-done | bytes 3488 | tf_op jit(solution)/shard_map/ppermute | solution.py:21
  284.2 4.3 %collective-permute-done.41 = f32[3,12,12,2]{3,2,1,0:T(8,128)S(1)} collective-permute-done((f32[3,12,12,2]{3,2,1,0:T(8,128)S(1)}, f32[3,12,12,2]{3,2,1,0:T(8,128)S(1)}, u32[]{:S(2)}, u32[]{:S(2)}) %collective-permute-start.41) | collective-permute-done | bytes 3488 | tf_op jit(solution)/shard_map/ppermute | solution.py:24
  (246 shorter events, 168.0 us)
Async XLA Ops:
  0.8 32.4 %collective-permute-start = (f32[2,2,16,128]{3,2,1,0:T(8,128)S(1)}, f32[2,2,16,128]{3,2,1,0:T(8,128)S(1)}, u32[]{:S(2)}, u32[]{:S(2)}) collective-permute-start(f32[2,2,16,128]{3,2,1,0:T(8,128)S(1)} %get-tuple-element.27), channel_id=1, source_target_pairs={{0,64},{64,128},{128,192},{192,256},{256,320},{320,384},{384,448},... | collective-permute-start | bytes 98312 | tf_op jit(solution)/shard_map/ppermute | solution.py:21
  5.3 27.9 %collective-permute-start.1 = (f32[2,2,16,128]{3,2,1,0:T(8,128)S(1)}, f32[2,2,16,128]{3,2,1,0:T(8,128)S(1)}, u32[]{:S(2)}, u32[]{:S(2)}) collective-permute-start(f32[2,2,16,128]{3,2,1,0:T(8,128)S(1)} %get-tuple-element.28), channel_id=1, source_target_pairs={{64,0},{128,64},{192,128},{256,192},{320,256},{384,320},{448,384},... | collective-permute-start | bytes 98312 | tf_op jit(solution)/shard_map/ppermute | solution.py:24
  40.3 10.0 %collective-permute-start.4 = (f32[2,20,20,2]{3,0,2,1:T(2,128)S(1)}, f32[2,20,20,2]{3,0,2,1:T(2,128)S(1)}, u32[]{:S(2)}, u32[]{:S(2)}) collective-permute-start(f32[2,20,20,2]{3,0,2,1:T(2,128)S(1)} %get-tuple-element.16), channel_id=1, source_target_pairs={{0,1},{1,2},{2,3},{3,4},{4,5},{5,6},{6,7},{8,9},{9,10},{10,11},{11... | collective-permute-start | bytes 19208 | tf_op jit(solution)/shard_map/ppermute | solution.py:21
  41.7 12.5 %collective-permute-start.5 = (f32[2,20,20,2]{3,0,2,1:T(2,128)S(1)}, f32[2,20,20,2]{3,0,2,1:T(2,128)S(1)}, u32[]{:S(2)}, u32[]{:S(2)}) collective-permute-start(f32[2,20,20,2]{3,0,2,1:T(2,128)S(1)} %get-tuple-element.17), channel_id=1, source_target_pairs={{1,0},{2,1},{3,2},{4,3},{5,4},{6,5},{7,6},{9,8},{10,9},{11,10},{12... | collective-permute-start | bytes 19208 | tf_op jit(solution)/shard_map/ppermute | solution.py:24
  81.8 7.3 %collective-permute-start.9 = (f32[2,12,2,64]{3,2,1,0:T(2,128)S(1)}, f32[2,12,2,64]{3,2,1,0:T(2,128)S(1)}, u32[]{:S(2)}, u32[]{:S(2)}) collective-permute-start(f32[2,12,2,64]{3,2,1,0:T(2,128)S(1)} %get-tuple-element.42), channel_id=1, source_target_pairs={{8,0},{16,8},{24,16},{32,24},{40,32},{48,40},{56,48},{9,1},{17,9},... | collective-permute-start | bytes 36872 | tf_op jit(solution)/shard_map/ppermute | solution.py:24
  89.4 6.6 %collective-permute-start.10 = (f32[2,12,12,2]{3,0,2,1:T(2,128)S(1)}, f32[2,12,12,2]{3,0,2,1:T(2,128)S(1)}, u32[]{:S(2)}, u32[]{:S(2)}) collective-permute-start(f32[2,12,12,2]{3,0,2,1:T(2,128)S(1)} %get-tuple-element.33), channel_id=1, source_target_pairs={{0,1},{1,2},{2,3},{3,4},{4,5},{5,6},{6,7},{8,9},{9,10},{10,11},{11... | collective-permute-start | bytes 6920 | tf_op jit(solution)/shard_map/ppermute | solution.py:21
  92.7 8.2 %collective-permute-start.11 = (f32[2,12,12,2]{3,0,2,1:T(2,128)S(1)}, f32[2,12,12,2]{3,0,2,1:T(2,128)S(1)}, u32[]{:S(2)}, u32[]{:S(2)}) collective-permute-start(f32[2,12,12,2]{3,0,2,1:T(2,128)S(1)} %get-tuple-element.34), channel_id=1, source_target_pairs={{1,0},{2,1},{3,2},{4,3},{5,4},{6,5},{7,6},{9,8},{10,9},{11,10},{12... | collective-permute-start | bytes 6920 | tf_op jit(solution)/shard_map/ppermute | solution.py:24
  104.4 6.0 %collective-permute-start.12 = (f32[2,2,4,32]{3,2,1,0:T(4,128)S(1)}, f32[2,2,4,32]{3,2,1,0:T(4,128)S(1)}, u32[]{:S(2)}, u32[]{:S(2)}) collective-permute-start(f32[2,2,4,32]{3,2,1,0:T(4,128)S(1)} %get-tuple-element.69), channel_id=1, source_target_pairs={{0,64},{64,128},{128,192},{192,256},{256,320},{320,384},{384,448},... | collective-permute-start | bytes 6152 | tf_op jit(solution)/shard_map/ppermute | solution.py:21
  113.4 6.0 %collective-permute-start.14 = (f32[2,8,2,32]{3,2,1,0:T(2,128)S(1)}, f32[2,8,2,32]{3,2,1,0:T(2,128)S(1)}, u32[]{:S(2)}, u32[]{:S(2)}) collective-permute-start(f32[2,8,2,32]{3,2,1,0:T(2,128)S(1)} %get-tuple-element.63), channel_id=1, source_target_pairs={{0,8},{8,16},{16,24},{24,32},{32,40},{40,48},{48,56},{1,9},{9,17},... | collective-permute-start | bytes 12296 | tf_op jit(solution)/shard_map/ppermute | solution.py:21
  122.7 6.5 %collective-permute-start.16 = (f32[2,8,8,2]{3,2,1,0:T(8,128)S(1)}, f32[2,8,8,2]{3,2,1,0:T(8,128)S(1)}, u32[]{:S(2)}, u32[]{:S(2)}) collective-permute-start(f32[2,8,8,2]{3,2,1,0:T(8,128)S(1)} %get-tuple-element.53), channel_id=1, source_target_pairs={{0,1},{1,2},{2,3},{3,4},{4,5},{5,6},{6,7},{8,9},{9,10},{10,11},{11... | collective-permute-start | bytes 3080 | tf_op jit(solution)/shard_map/ppermute | solution.py:21
  127.3 5.8 %collective-permute-start.17 = (f32[2,8,8,2]{3,2,1,0:T(8,128)S(1)}, f32[2,8,8,2]{3,2,1,0:T(8,128)S(1)}, u32[]{:S(2)}, u32[]{:S(2)}) collective-permute-start(f32[2,8,8,2]{3,2,1,0:T(8,128)S(1)} %get-tuple-element.54), channel_id=1, source_target_pairs={{1,0},{2,1},{3,2},{4,3},{5,4},{6,5},{7,6},{9,8},{10,9},{11,10},{12... | collective-permute-start | bytes 3080 | tf_op jit(solution)/shard_map/ppermute | solution.py:24
  134.0 6.9 %collective-permute-start.18 = (f32[2,2,2,16]{3,2,1,0:T(2,128)S(1)}, f32[2,2,2,16]{3,2,1,0:T(2,128)S(1)}, u32[]{:S(2)}, u32[]{:S(2)}) collective-permute-start(f32[2,2,2,16]{3,2,1,0:T(2,128)S(1)} %pad_maximum_fusion.43), channel_id=1, source_target_pairs={{0,64},{64,128},{128,192},{192,256},{256,320},{320,384},{384,448},... | collective-permute-start | bytes 1544 | tf_op jit(solution)/shard_map/ppermute | solution.py:21
  143.8 6.0 %collective-permute-start.20 = (f32[2,6,2,16]{3,2,1,0:T(2,128)S(1)}, f32[2,6,2,16]{3,2,1,0:T(2,128)S(1)}, u32[]{:S(2)}, u32[]{:S(2)}) collective-permute-start(f32[2,6,2,16]{3,2,1,0:T(2,128)S(1)} %pad_maximum_fusion.40), channel_id=1, source_target_pairs={{0,8},{8,16},{16,24},{24,32},{32,40},{40,48},{48,56},{1,9},{9,17},... | collective-permute-start | bytes 4616 | tf_op jit(solution)/shard_map/ppermute | solution.py:21
  165.2 20.5 %all-to-all-start = ((f32[64,1,2]{2,1,0:T(1,128)}), f32[64,1,2]{2,1,0:T(1,128)S(1)}, u32[]{:S(2)}, u32[]{:S(2)}) async-start(f32[64,1,2]{2,1,0:T(1,128)} %broadcast_in_dim.24), calls=%async_computation | async-start | bytes 65536 | tf_op jit(solution)/shard_map/all_to_all | solution.py:37
  186.4 16.9 %all-to-all-start.1 = ((f32[16,1,128]{2,1,0:T(1,128)}), f32[16,1,128]{2,1,0:T(1,128)S(1)}, u32[]{:S(2)}, u32[]{:S(2)}) async-start(f32[16,1,128]{2,1,0:T(1,128)} %reshape.429), calls=%async_computation.1 | async-start | bytes 16384 | tf_op jit(solution)/shard_map/all_to_all | solution.py:37
  227.0 5.9 %collective-permute-start.29 = (f32[3,6,6,2]{3,2,1,0:T(8,128)S(1)}, f32[3,6,6,2]{3,2,1,0:T(8,128)S(1)}, u32[]{:S(2)}, u32[]{:S(2)}) collective-permute-start(f32[3,6,6,2]{3,2,1,0:T(8,128)S(1)} %get-tuple-element.48), channel_id=1, source_target_pairs={{1,0},{2,1},{3,2},{4,3},{5,4},{6,5},{7,6},{9,8},{10,9},{11,10},{12... | collective-permute-start | bytes 2600 | tf_op jit(solution)/shard_map/ppermute | solution.py:24
  233.6 6.0 %collective-permute-start.30 = (f32[3,2,4,32]{3,2,1,0:T(4,128)S(1)}, f32[3,2,4,32]{3,2,1,0:T(4,128)S(1)}, u32[]{:S(2)}, u32[]{:S(2)}) collective-permute-start(f32[3,2,4,32]{3,2,1,0:T(4,128)S(1)} %get-tuple-element.67), channel_id=1, source_target_pairs={{0,64},{64,128},{128,192},{192,256},{256,320},{320,384},{384,448},... | collective-permute-start | bytes 9224 | tf_op jit(solution)/shard_map/ppermute | solution.py:21
  251.9 6.5 %collective-permute-start.35 = (f32[3,8,8,2]{3,2,1,0:T(8,128)S(1)}, f32[3,8,8,2]{3,2,1,0:T(8,128)S(1)}, u32[]{:S(2)}, u32[]{:S(2)}) collective-permute-start(f32[3,8,8,2]{3,2,1,0:T(8,128)S(1)} %get-tuple-element.41), channel_id=1, source_target_pairs={{1,0},{2,1},{3,2},{4,3},{5,4},{6,5},{7,6},{9,8},{10,9},{11,10},{12... | collective-permute-start | bytes 4616 | tf_op jit(solution)/shard_map/ppermute | solution.py:24
  259.2 5.6 %collective-permute-start.36 = (f32[3,2,8,64]{3,2,1,0:T(8,128)S(1)}, f32[3,2,8,64]{3,2,1,0:T(8,128)S(1)}, u32[]{:S(2)}, u32[]{:S(2)}) collective-permute-start(f32[3,2,8,64]{3,2,1,0:T(8,128)S(1)} %get-tuple-element.35), channel_id=1, source_target_pairs={{0,64},{64,128},{128,192},{192,256},{256,320},{320,384},{384,448},... | collective-permute-start | bytes 36872 | tf_op jit(solution)/shard_map/ppermute | solution.py:21
  275.3 8.8 %collective-permute-start.40 = (f32[3,12,12,2]{3,2,1,0:T(8,128)S(1)}, f32[3,12,12,2]{3,2,1,0:T(8,128)S(1)}, u32[]{:S(2)}, u32[]{:S(2)}) collective-permute-start(f32[3,12,12,2]{3,2,1,0:T(8,128)S(1)} %get-tuple-element.25), channel_id=1, source_target_pairs={{0,1},{1,2},{2,3},{3,4},{4,5},{5,6},{6,7},{8,9},{9,10},{10,11},{11... | collective-permute-start | bytes 10376 | tf_op jit(solution)/shard_map/ppermute | solution.py:21
  277.5 10.9 %collective-permute-start.41 = (f32[3,12,12,2]{3,2,1,0:T(8,128)S(1)}, f32[3,12,12,2]{3,2,1,0:T(8,128)S(1)}, u32[]{:S(2)}, u32[]{:S(2)}) collective-permute-start(f32[3,12,12,2]{3,2,1,0:T(8,128)S(1)} %get-tuple-element.26), channel_id=1, source_target_pairs={{1,0},{2,1},{3,2},{4,3},{5,4},{6,5},{7,6},{9,8},{10,9},{11,10},{12... | collective-permute-start | bytes 10376 | tf_op jit(solution)/shard_map/ppermute | solution.py:24
  292.8 5.4 %collective-permute-start.43 = (f32[3,2,16,128]{3,2,1,0:T(8,128)S(1)}, f32[3,2,16,128]{3,2,1,0:T(8,128)S(1)}, u32[]{:S(2)}, u32[]{:S(2)}) collective-permute-start(f32[3,2,16,128]{3,2,1,0:T(8,128)S(1)} %get-tuple-element.19), channel_id=1, source_target_pairs={{64,0},{128,64},{192,128},{256,192},{320,256},{384,320},{448,384},... | collective-permute-start | bytes 147464 | tf_op jit(solution)/shard_map/ppermute | solution.py:24
  307.4 5.3 %collective-permute-start.46 = (f32[3,20,20,2]{2,3,1,0:T(2,128)S(1)}, f32[3,20,20,2]{2,3,1,0:T(2,128)S(1)}, u32[]{:S(2)}, u32[]{:S(2)}) collective-permute-start(f32[3,20,20,2]{2,3,1,0:T(2,128)S(1)} %copy.212), channel_id=1, source_target_pairs={{0,1},{1,2},{2,3},{3,4},{4,5},{5,6},{6,7},{8,9},{9,10},{10,11},{11... | collective-permute-start | bytes 28808 | tf_op jit(solution)/shard_map/ppermute | solution.py:21
  311.2 5.7 %collective-permute-start.47 = (f32[3,20,20,2]{2,3,1,0:T(2,128)S(1)}, f32[3,20,20,2]{2,3,1,0:T(2,128)S(1)}, u32[]{:S(2)}, u32[]{:S(2)}) collective-permute-start(f32[3,20,20,2]{2,3,1,0:T(2,128)S(1)} %copy.213), channel_id=1, source_target_pairs={{1,0},{2,1},{3,2},{4,3},{5,4},{6,5},{7,6},{9,8},{10,9},{11,10},{12... | collective-permute-start | bytes 28808 | tf_op jit(solution)/shard_map/ppermute | solution.py:24
  (28 other events, 128.0 us)
where the time goes:
time: 323 us; the launch traced here: 321 us
  starting transfers between devices  142 us (44%)
  waiting for transfers between devices  118 us (37%)
  local copies, waits for them, and re-layouts  31.9 us (10%)
  other arithmetic  22.7 us (7%)
  between operations  3.33 us (1%)
    ppermute x24, waiting for transfers between devices, with_halo(): lax.ppermute(lax.slice_in_dim(block, 0, width, axis=dim), axis, backward)  83 us
    ppermute x24, starting transfers between devices, with_halo(): lax.ppermute(lax.slice_in_dim(block, block.shape[dim] - width, None, axis...  74.6 us
    ppermute x24, starting transfers between devices, with_halo(): lax.ppermute(lax.slice_in_dim(block, 0, width, axis=dim), axis, backward)  47.9 us
    reshape x4, local copies, waits for them, and re-layouts, coarsen(): values.reshape(size_x // block_x, block_x, size_y // block_y, block_y, si...  21.5 us
    all_to_all x2, starting transfers between devices, sent_to_all(): lax.all_to_all(jnp.broadcast_to(shard[None], (length, *shard.shape)), axi...  19.7 us
    all_to_all x2, waiting for transfers between devices, sent_to_all(): lax.all_to_all(jnp.broadcast_to(shard[None], (length, *shard.shape)), axi...  17.7 us
    ppermute x24, waiting for transfers between devices, with_halo(): lax.ppermute(lax.slice_in_dim(block, block.shape[dim] - width, None, axis...  17.2 us
    reduce_sum x6, other arithmetic, coarsen(): return shaped.mean(axis=(1, 3, 5))  8.58 us
  transfers between devices with their start and end apart: 50, of which 32 were waited for; matrix products, arithmetic and copies ran while one was open for 5% of the time, Pallas kernels for 0%

commit v1 on v0

v1 whole, which is shorter than its diff:
```python
import functools
import itertools
import math

import jax
import jax.numpy as jnp
import numpy as np
from jax import lax
from jax.experimental import pallas as pl
from jax.experimental.pallas import tpu as pltpu
from jax.sharding import PartitionSpec as P

MESH = pl.DeviceIdType.MESH
HI = lax.Precision.HIGHEST
LEVELS = 4
LANES = 128
RELAX = 2.0 / 3.0
SIZE = (16, 8, 4, 2)
DEPTH = (128, 64, 32, 16)
HALO = (3, 4, 4, 2)
ROW = (4, 4, 4, 2)
PLANES = tuple(n + 2 * r for n, r in zip(SIZE, HALO))
ROWS = (24, 16, 16, 8)
OFFSETS = [o for o in itertools.product((-1, 0, 1), repeat=3) if o != (0, 0, 0)]
FLAT = [o for o in OFFSETS if o[2] == 0]
TALL = [o for o in OFFSETS if o[2] != 0]


def iota(shape, axis):
    return lax.broadcasted_iota(jnp.int32, shape, axis)


def neighbour_sum(v):
    c = v[1:-1]
    rows, lanes = c.shape[1], c.shape[2]
    total = v[2:] + v[:-2]
    total = total + (pltpu.roll(c, 1, 1) + pltpu.roll(c, rows - 1, 1))
    return total + (pltpu.roll(c, 1, 2) + pltpu.roll(c, lanes - 1, 2))


def sweep(v, b, w):
    return v[1:-1] * (1.0 / 3.0) + w * (b + neighbour_sum(v))


def pair_planes(v):
    n = v.shape[0]
    halves = v.reshape(n // 2, 2, v.shape[1], v.shape[2])
    return halves[:, 0] + halves[:, 1]


def lanes_dot(v, table):
    planes, rows, lanes = v.shape
    out = jnp.dot(
        v.reshape(planes * rows, lanes), table, precision=HI, preferred_element_type=jnp.float32
    )
    return out.reshape(planes, rows, table.shape[1])


def refine_table(lanes, turn):
    fine = iota((LANES, lanes), 1)
    place = jnp.where(fine < turn, fine, fine - lanes)
    coarse = jnp.bitwise_and(place + 2 * LANES, 1)
    coarse = (place + 2 * LANES - coarse) // 2 % LANES
    return (iota((LANES, lanes), 0) == coarse).astype(jnp.float32)


def kernel(counts, b_hbm, d_hbm, tab_ref, out_ref, *refs):
    NX, NY, NZ = counts
    NXP = max(8, NX)
    it = iter(refs)
    eb, ed, e1, e2, e3, u2, u3, x3 = (next(it) for _ in range(8))
    zs = [next(it) for _ in range(7)]
    zr = [next(it) for _ in range(7)]
    bx = [next(it) for _ in range(4)]
    wx = [next(it) for _ in range(4)]
    vx = [next(it) for _ in range(4)]
    pair, fine0 = next(it), next(it)
    row0, row1, row2, g1, g2, g3 = (next(it) for _ in range(6))
    tally = next(it)
    send_sem, recv_sem, line_send, line_recv, in_sem = (next(it) for _ in range(5))

    gx, gy, gz = lax.axis_index("gx"), lax.axis_index("gy"), lax.axis_index("gz")

    places = {}
    for name, here, count in zip(("gx", "gy", "gz"), (gx, gy, gz), counts):
        places[name, 0] = here
        for step in range(1, count):
            moved = here + step
            places[name, step] = jnp.where(moved >= count, moved - count, moved)

    def device(offset):
        return tuple(
            places[name, step % count]
            for name, count, step in zip(("gx", "gy", "gz"), counts, offset)
        )

    for ref in (eb, ed, e1, e2, e3, u2, u3, x3, pair, *zs, *zr):
        ref[...] = jnp.zeros(ref.shape, jnp.float32)
    n = SIZE[0]
    loads = []
    for k, (src, dst) in enumerate(((b_hbm, eb), (d_hbm, ed))):
        load = pltpu.make_async_copy(
            src, dst.at[pl.ds(HALO[0], n), pl.ds(ROW[0], n)], in_sem.at[k]
        )
        load.start()
        loads.append(load)

    peers = set()
    for o in OFFSETS:
        peers.add(tuple(s % c for s, c in zip(o, counts)))
    for axis in range(3):
        for k in range(1, counts[axis]):
            peers.add(tuple(k if a == axis else 0 for a in range(3)))
    peers.discard((0, 0, 0))
    barrier = pltpu.get_barrier_semaphore()
    for o in sorted(peers):
        pl.semaphore_signal(barrier, inc=1, device_id=device(o), device_id_type=MESH)

    lane = iota((1, LANES), 1)
    low = jnp.bitwise_and(lane, 63)
    halve = (
        iota((LANES, LANES), 0) // 2 == iota((LANES, LANES), 1)
    ).astype(jnp.float32) * 0.5

    def coarsen_own(level, values, first):
        half = SIZE[level] // 2
        rows = values.shape[1]
        pair[0:half, 0:rows, :] = pair_planes(values)
        top = pair[0:half, pl.ds(first, 8, stride=2), :]
        top = top + pair[0:half, pl.ds(first + 1, 8, stride=2), :]
        return lanes_dot(top, halve)

    def pack(level, which, fields):
        r, bz = HALO[level], DEPTH[level]
        joined = len(fields) == 1
        for side in range(2):
            start = bz - r if side else 0
            acc = jnp.zeros((SIZE[level], LANES), jnp.float32)
            for x in range(SIZE[level]):
                for f, values in enumerate(fields):
                    place = f * 64 + x * r
                    shift = (place - start) % LANES
                    moved = values[x] if shift == 0 else pltpu.roll(values[x], shift, 1)
                    seat = low if joined else lane - f * 64
                    acc = jnp.where((seat >= x * r) & (seat < x * r + r), moved, acc)
            zs[which][side, :, :] = acc

    def unpack(level, which, f):
        n, r, bz = SIZE[level], HALO[level], DEPTH[level] % LANES
        planes = []
        for p in range(PLANES[level]):
            block, x = divmod(p - r + n, n)
            seat = f * 64 + x * r
            down = (LANES - r - seat) % LANES
            up = (bz - seat) % LANES
            below, above = zr[which][0, block], zr[which][1, block]
            below = pltpu.roll(below, down, 1) if down else below
            above = pltpu.roll(above, up, 1) if up else above
            inner = jnp.where((lane >= bz) & (lane < bz + r), above, 0.0)
            planes.append(jnp.where(lane >= LANES - r, below, inner))
        return jnp.stack(planes, axis=0)

    def span(step, n, r):
        return ((0, n), (n - r, r), (0, r))[step]

    unsent = {}

    def drain(sem, rows):
        pltpu.make_async_copy(tally.at[pl.ds(0, rows)], tally.at[pl.ds(0, rows)], sem).wait()

    def sent(turn_set):
        if turn_set in unsent:
            drain(send_sem.at[turn_set], unsent.pop(turn_set))

    def exchange(level, which, blocks, turn_set):
        n, r, row = SIZE[level], HALO[level], ROW[level]
        sent(turn_set)
        sems = dict(send_sem=send_sem.at[turn_set], recv_sem=recv_sem.at[turn_set])
        copies, rows = [], 0
        for o in TALL:
            sy, cy = span(o[1], n, r)
            up = o[2] > 0
            rows += cy
            copies.append(
                pltpu.make_async_remote_copy(
                    src_ref=zs[which].at[1 if up else 0, pl.ds(sy, cy)],
                    dst_ref=zr[which].at[
                        0 if up else 1, 1 - o[0], pl.ds(row + sy - o[1] * n, cy)
                    ],
                    device_id=device(o),
                    device_id_type=MESH,
                    **sems,
                )
            )
        for o in FLAT:
            sx, cx = span(o[0], n, r)
            sy, cy = span(o[1], n, r)
            for block in blocks:
                rows += cx * cy
                copies.append(
                    pltpu.make_async_remote_copy(
                        src_ref=block.at[pl.ds(r + sx, cx), pl.ds(row + sy, cy)],
                        dst_ref=block.at[
                            pl.ds(r + sx - o[0] * n, cx), pl.ds(row + sy - o[1] * n, cy)
                        ],
                        device_id=device(o),
                        device_id_type=MESH,
                        **sems,
                    )
                )
        for copy in copies:
            copy.start()
        unsent[turn_set] = rows
        return turn_set, rows

    def finish(pending):
        drain(recv_sem.at[pending[0]], pending[1])

    def domain(level):
        n, r, row, bz = SIZE[level], HALO[level], ROW[level], DEPTH[level]
        lanes = 256 if level == 0 else LANES
        px = iota((PLANES[level], 1, 1), 0) - r
        py = iota((1, ROWS[level], 1), 1) - row
        pz = iota((1, 1, lanes), 2)
        pz = jnp.where(pz < bz + 32, pz, pz - lanes)
        ok = None
        for p, here, count, size in ((px, gx, NX, n), (py, gy, NY, n), (pz, gz, NZ, bz)):
            at = p + here * size
            good = (p >= -r) & (p < size + r) & (at >= 0) & (at < count * size)
            ok = good if ok is None else ok & good
        return ok

    def presmooth(level, b, d):
        n, r = SIZE[level], HALO[level]
        diag = 6.0 + d
        w = jnp.where(domain(level), RELAX / diag, 0.0)
        bx[level][...] = b
        wx[level][...] = w
        v = w * b
        v = sweep(v, b[1:-1], w[1:-1])
        vx[level][...] = v
        near = v[r - 2 : r + n]
        own = near[1:-1]
        return (b[r : r + n] - diag[r : r + n] * own + neighbour_sum(near))[:, :, :LANES]

    own_damping = []
    for load in loads:
        load.wait()
    d_own = ed[pl.ds(HALO[0], n), pl.ds(ROW[0], n), :]
    pack(0, 0, (eb[pl.ds(HALO[0], n), pl.ds(ROW[0], n), :], d_own))
    pl.semaphore_wait(barrier, len(peers))
    copies = exchange(0, 0, (eb, ed), 0)

    values = d_own
    for level in range(LEVELS - 1):
        coarse = coarsen_own(level, values, 0)
        own_damping.append(coarse)
        values = coarse
    d_last = own_damping[-1]
    own_nodes = (iota((8, LANES), 0) < SIZE[3]) & (iota((8, LANES), 1) < DEPTH[3])
    last_scale = 0.25 ** (LEVELS - 1) / (SIZE[3] * SIZE[3] * DEPTH[3])

    def block_mean(planes, good):
        total = jnp.where(good, sum(planes[k] for k in range(planes.shape[0])), 0.0)
        total = jnp.sum(jnp.sum(total, axis=0, keepdims=True), axis=1, keepdims=True)
        return total * last_scale

    damping_mean = block_mean(d_last, own_nodes)

    finish(copies)
    b0 = jnp.concatenate([eb[...], unpack(0, 0, 0)], axis=2)
    d0 = jnp.concatenate([ed[...], unpack(0, 0, 1)], axis=2)
    remainder = presmooth(0, b0, d0)

    hidden = None
    for level, block in ((1, e1), (2, e2), (3, e3)):
        n, r, row, bz = SIZE[level], HALO[level], ROW[level], DEPTH[level]
        coarse = coarsen_own(level - 1, remainder, ROW[level - 1])
        both = jnp.where(lane < 64, coarse, pltpu.roll(own_damping[level - 1], 64, 2))
        both = both[:, :n]
        block[pl.ds(r, n), pl.ds(row, n), :] = both
        pack(level, level, (both,))
        copies = exchange(level, level, (block,), (0, 1, 2, 1)[level])
        finish(copies)
        e = block[...]
        b = jnp.where(lane < bz, e, unpack(level, level, 0))
        d = jnp.where(lane < bz, pltpu.roll(e, 64, 2), unpack(level, level, 1))
        remainder = presmooth(level, b, d)
        if level >= 2:
            own = vx[level][pl.ds(r - 1, n), pl.ds(row, n), :]
            which = level + 2
            target = (u2, u3)[level - 2]
            target[pl.ds(r, n), pl.ds(row, n), :] = own
            pack(level, which, (own,))
            if hidden is not None:
                finish(hidden)
            hidden = exchange(level, which, (target,), (0, 2)[level - 2])

    source = block_mean(
        remainder,
        (iota((8, LANES), 0) >= ROW[3])
        & (iota((8, LANES), 0) < ROW[3] + SIZE[3])
        & (iota((8, LANES), 1) < DEPTH[3]),
    )

    def send_line(axis, src, dst):
        here, count = (gx, gy, gz)[axis], counts[axis]
        for k in range(1, count):
            offset = tuple(k if a == axis else 0 for a in range(3))
            pltpu.make_async_remote_copy(
                src_ref=src.at[pl.ds(0, 1)],
                dst_ref=dst.at[pl.ds(here, 1)],
                send_sem=line_send.at[axis],
                recv_sem=line_recv.at[axis],
                device_id=device(offset),
                device_id_type=MESH,
            ).start()

    def finish_line(axis):
        drain(line_recv.at[axis], counts[axis] - 1)

    def line_rows(axis, own, dst):
        here, count = (gx, gy, gz)[axis], counts[axis]
        rows = iota(dst.shape, 0)
        got = jnp.where(rows == here, own, dst[...])
        return jnp.where(rows < count, got, 0.0), rows

    own0 = jnp.where(lane < 64, source, damping_mean)
    row0[...] = jnp.broadcast_to(own0, (8, LANES))
    send_line(2, row0, g1)
    finish_line(2)
    got, rows = line_rows(2, own0, g1)
    own1 = jnp.sum(
        jnp.where((lane >= 64) | (lane % NZ == rows), got, 0.0), axis=0, keepdims=True
    )
    row1[...] = jnp.broadcast_to(own1, (8, LANES))
    send_line(1, row1, g2)
    finish_line(1)
    got, rows = line_rows(1, own1, g2)
    own2 = jnp.sum(
        jnp.where((lane >= 64) | (lane // NZ == rows), got, 0.0), axis=0, keepdims=True
    )
    row2[...] = jnp.broadcast_to(own2, (8, LANES))
    send_line(0, row2, g3)
    finish(hidden)
    finish_line(0)
    got, rows = line_rows(0, own2, g3)
    mean = jnp.sum(got, axis=0, keepdims=True) * (1.0 / (NX * NY * NZ))
    mean = jnp.where(lane < 64, pltpu.roll(mean, 64, 1), 0.0)
    table_x = tab_ref[0:NXP, 0:NXP]
    table_yz = tab_ref[pl.ds(16, LANES), :]
    eigen = tab_ref[pl.ds(16 + LANES, NXP), :]
    dot = functools.partial(jnp.dot, precision=HI, preferred_element_type=jnp.float32)
    spectrum = dot(dot(table_x, jnp.where(lane < NY * NZ, got, 0.0)), table_yz)
    spectrum = spectrum / (eigen + mean)
    coarse = dot(dot(table_x, spectrum), table_yz)

    pick = iota((8, NXP), 1) == gx - 1 + iota((8, NXP), 0) // 2
    along_x = dot(pick.astype(jnp.float32), coarse)
    wanted = iota((8, LANES), 1) // NZ == gy - 1 + iota((8, LANES), 0) // 2
    spread = jnp.stack(
        [
            jnp.where(wanted, jnp.broadcast_to(along_x[p : p + 1], (8, LANES)), 0.0)
            for p in range(PLANES[3])
        ],
        axis=0,
    )
    lane_to = iota((LANES, LANES), 1)
    block_z = jnp.where(lane_to < DEPTH[3], 0, jnp.where(lane_to < 64, 1, -1))
    seat = iota((LANES, LANES), 0) % NZ == gz + block_z
    correction = lanes_dot(spread, seat.astype(jnp.float32))

    def halo_values(level, block, which):
        return jnp.where(lane < DEPTH[level], block[...], unpack(level, which, 0))

    def postsmooth(level, v, start):
        for _ in range(2):
            start = start + 1
            count = v.shape[0] - 2
            v = sweep(v, bx[level][pl.ds(start, count)], wx[level][pl.ds(start, count)])
        return v

    def in_domain(level, v):
        return jnp.where(domain(level), v, 0.0)

    v = in_domain(3, halo_values(3, u3, 5) + correction)
    v = postsmooth(3, v, 0)
    own = v[:, ROW[3] : ROW[3] + SIZE[3]]
    x3[pl.ds(HALO[3], SIZE[3]), pl.ds(ROW[3], SIZE[3]), :] = own
    pack(3, 6, (own,))
    copies = exchange(3, 6, (x3,), 0)
    finish(copies)
    v = in_domain(3, halo_values(3, x3, 6))

    def refined(level, v, first):
        lanes = 256 if level == 0 else LANES
        table = refine_table(lanes, DEPTH[level] + 32)
        planes = v.shape[0]
        wide = lanes_dot(v, table)
        count = ROWS[level] // 2
        parts = []
        for half in range(lanes // LANES):
            piece = wide[:, first : first + count, half * LANES : (half + 1) * LANES]
            fine0[0:planes, pl.ds(0, count, stride=2), :] = piece
            fine0[0:planes, pl.ds(1, count, stride=2), :] = piece
            parts.append(fine0[0:planes, 0 : ROWS[level], :])
        full = parts[0] if len(parts) == 1 else jnp.concatenate(parts, axis=2)
        full = jnp.broadcast_to(full[:, None], (planes, 2, ROWS[level], lanes))
        return full.reshape(2 * planes, ROWS[level], lanes)

    v = halo_values(2, u2, 4) + refined(2, v, 0)
    v = postsmooth(2, in_domain(2, v), 0)
    correction = refined(1, v, ROW[2] - 2)
    v = vx[1][...] + correction[1:-1]
    v = postsmooth(1, v, 1)
    correction = refined(0, v, ROW[1] - 2)
    v = vx[0][...] + correction
    v = postsmooth(0, v, 1)
    for axis in range(3):
        drain(line_send.at[axis], counts[axis] - 1)
    for turn_set in list(unsent):
        sent(turn_set)
    out_ref[...] = v[:, ROW[0] : ROW[0] + SIZE[0], :LANES]


def tables(counts):
    def sine(points):
        index = np.arange(1, points + 1)
        return math.sqrt(2.0 / (points + 1)) * np.sin(
            math.pi * index[:, None] * index[None, :] / (points + 1)
        )

    def eigen(points, spacing):
        index = np.arange(1, points + 1)
        return (2.0 - 2.0 * np.cos(math.pi * index / (points + 1))) / (spacing * spacing)

    nx, ny, nz = counts
    out = np.zeros((16 + LANES + 16, LANES))
    out[:nx, :nx] = sine(nx)
    out[16 : 16 + ny * nz, : ny * nz] = np.kron(sine(ny), sine(nz))
    plane = eigen(ny, 16.0)[:, None] + eigen(nz, 128.0)[None, :]
    out[16 + LANES :] = 1.0
    out[16 + LANES : 16 + LANES + nx, : ny * nz] = eigen(nx, 16.0)[:, None] + plane.reshape(1, -1)
    return out.astype(np.float32)


def solution(mesh):
    counts = tuple(mesh.shape[a] for a in ("gx", "gy", "gz"))
    NXP = max(8, counts[0])
    f32 = jnp.float32

    def local(divergence, damping):
        ext = [(p, r, LANES) for p, r in zip(PLANES, ROWS)]
        levels = (0, 1, 2, 3, 2, 3, 3)
        wide = [(p, r, 256 if k == 0 else LANES) for k, (p, r) in enumerate(zip(PLANES, ROWS))]
        inner = [(p - 2, r, z) for p, r, z in wide]
        shapes = [ext[0], ext[0], ext[1], ext[2], ext[3], ext[2], ext[3], ext[3]]
        shapes += [(2, SIZE[k], LANES) for k in levels]
        shapes += [(2, 3, ROWS[k], LANES) for k in levels]
        shapes += wide + wide + inner
        shapes += [(8, 24, LANES), (12, 24, LANES)]
        shapes += [(8, LANES)] * 3
        shapes += [(8, LANES), (8, LANES), (NXP, LANES), (2048, LANES)]
        dma = pltpu.SemaphoreType.DMA
        sems = [dma((3,)), dma((3,)), dma((3,)), dma((3,)), dma((2,))]
        return pl.pallas_call(
            functools.partial(kernel, counts),
            out_shape=jax.ShapeDtypeStruct(divergence.shape, f32),
            in_specs=[
                pl.BlockSpec(memory_space=pl.ANY),
                pl.BlockSpec(memory_space=pl.ANY),
                pl.BlockSpec(memory_space=pltpu.VMEM),
            ],
            out_specs=pl.BlockSpec(memory_space=pltpu.VMEM),
            scratch_shapes=[pltpu.VMEM(s, f32) for s in shapes] + sems,
            compiler_params=pltpu.CompilerParams(
                collective_id=0, has_side_effects=True, vmem_limit_bytes=48 * 1024 * 1024
            ),
            name="vcycle",
        )(divergence, damping, jnp.asarray(tables(counts)))

    spec = P("gx", "gy", "gz")
    return jax.shard_map(
        local, mesh=mesh, in_specs=(spec, spec), out_specs=spec, check_vma=False
    )
```

time: 323 us -> 71.5 us (0.22)
  starting transfers between devices: 142 us -> 0 us
  waiting for transfers between devices: 118 us -> 0 us
  Pallas kernels: 0 us -> 67.9 us
  local copies, waits for them, and re-layouts: 31.9 us -> 3.35 us
  other arithmetic: 22.7 us -> 0 us
  between operations: 3.33 us -> 0.01 us
    ppermute x48 -> x0, starting transfers between devices: 123 us -> none  [the longest x24 74.6 us: with_halo(): lax.ppermute(lax.slice_in_dim(block, block.shape[dim] - width, None, axis...]
    ppermute x48 -> x0, waiting for transfers between devices: 100 us -> none  [the longest x24 83 us: with_halo(): lax.ppermute(lax.slice_in_dim(block, 0, width, axis=dim), axis, backward)]
    pallas_call x0 -> x1, Pallas kernels: none -> 67.9 us  [local(): pl.pallas_call(functools.partial(kernel, counts), out_shape=jax.ShapeDtyp...]
    reshape x11 -> x0, local copies, waits for them, and re-layouts: 22.7 us -> none  [the longest x4 21.5 us: coarsen(): values.reshape(size_x // block_x, block_x, size_y // block_y, block_y, si...]
    all_to_all x2 -> x0, starting transfers between devices: 19.7 us -> none  [sent_to_all(): lax.all_to_all(jnp.broadcast_to(shard[None], (length, *shard.shape)), axi...]
    all_to_all x2 -> x0, waiting for transfers between devices: 17.7 us -> none  [sent_to_all(): lax.all_to_all(jnp.broadcast_to(shard[None], (length, *shard.shape)), axi...]
    reduce_sum x8 -> x0, other arithmetic: 9.96 us -> none  [the longest x6 8.58 us: coarsen(): return shaped.mean(axis=(1, 3, 5))]
    mul x12 -> x0, other arithmetic: 4.59 us -> none  [the longest x8 2.98 us: deep_postsmooth(): relaxed_sweep(trimmed(current, 1), current, trimmed(source_ext, margin),...]
  transfers between devices with their start and end apart: 50 -> 0, of which waited for: 32 -> 0; matrix products, arithmetic and copies ran while one was open for 5% -> 0% of each run, Pallas kernels for 0% -> 0%
where the time goes in v1:
time: 71.5 us; the launch traced here: 71.3 us
  Pallas kernels  67.9 us (95%)
  local copies, waits for them, and re-layouts  3.35 us (5%)
    pallas_call x1, Pallas kernels, local(): pl.pallas_call(functools.partial(kernel, counts), out_shape=jax.ShapeDtyp...  67.9 us
    unnamed x7, local copies, waits for them, and re-layouts  3.35 us

profile of v1, /device:TPU:1, one launch (start us, length us, event | category | flops | bytes accessed | tf_op | source)
XLA Modules:
  0.0 71.3 jit_solution(5943736720924045917)
XLA Ops:
  0.0 0.0 copy-start
  0.0 0.9 %copy-done = f32[16,16,128]{2,1,0:T(8,128)S(1)} copy-done((f32[16,16,128]{2,1,0:T(8,128)S(1)}, f32[16,16,128]{2,1,0:T(8,128)}, u32[]{:S(2)}) %copy-start) | copy-done | bytes 131096
  0.9 0.0 copy-start.1
  0.9 0.9 %copy-done.1 = f32[16,16,128]{2,1,0:T(8,128)S(1)} copy-done((f32[16,16,128]{2,1,0:T(8,128)S(1)}, f32[16,16,128]{2,1,0:T(8,128)}, u32[]{:S(2)}) %copy-start.1) | copy-done | bytes 131096
  1.8 0.0 copy-start.2
  1.8 0.9 %copy-done.2 = f32[160,128]{1,0:T(8,128)S(1)} copy-done((f32[160,128]{1,0:T(8,128)S(1)}, f32[160,128]{1,0:T(8,128)}, u32[]{:S(2)}) %copy-start.2) | copy-done | bytes 81944
  2.7 67.9 %vcycle.1 = f32[16,16,128]{2,1,0:T(8,128)S(1)} custom-call(f32[16,16,128]{2,1,0:T(8,128)S(1)} %copy-done, f32[16,16,128]{2,1,0:T(8,128)S(1)} %copy-done.1, f32[160,128]{1,0:T(8,128)S(1)} %copy-done.2), custom_call_target="tpu_custom_call" | custom-call | tf_op jit(solution)/shard_map/vcycle/pallas_call | solution.py:466
  70.6 0.7 copy.5
Async XLA Ops:
  0.0 0.9 %copy-start = (f32[16,16,128]{2,1,0:T(8,128)S(1)}, f32[16,16,128]{2,1,0:T(8,128)}, u32[]{:S(2)}) copy-start(f32[16,16,128]{2,1,0:T(8,128)} %b_hbm.1) | copy-start | bytes 393220
  0.9 0.9 %copy-start.1 = (f32[16,16,128]{2,1,0:T(8,128)S(1)}, f32[16,16,128]{2,1,0:T(8,128)}, u32[]{:S(2)}) copy-start(f32[16,16,128]{2,1,0:T(8,128)} %d_hbm.1) | copy-start | bytes 393220
  1.8 0.9 %copy-start.2 = (f32[160,128]{1,0:T(8,128)S(1)}, f32[160,128]{1,0:T(8,128)}, u32[]{:S(2)}) copy-start(f32[160,128]{1,0:T(8,128)} %constant.2.clone.tab_ref) | copy-start | bytes 245764

commit v2 on v1

--- a/solution.py
+++ b/solution.py
@@ -17,10 +17,11 @@
 RELAX = 2.0 / 3.0
 SIZE = (16, 8, 4, 2)
 DEPTH = (128, 64, 32, 16)
-HALO = (3, 4, 4, 2)
-ROW = (4, 4, 4, 2)
+HALO = (3, 6, 4, 2)
+ROW = (4, 8, 4, 2)
 PLANES = tuple(n + 2 * r for n, r in zip(SIZE, HALO))
-ROWS = (24, 16, 16, 8)
+ROWS = (24, 24, 16, 8)
+PITCH = (64, 64, 32, 64)
 OFFSETS = [o for o in itertools.product((-1, 0, 1), repeat=3) if o != (0, 0, 0)]
 FLAT = [o for o in OFFSETS if o[2] == 0]
 TALL = [o for o in OFFSETS if o[2] != 0]
@@ -64,16 +65,16 @@
     return (iota((LANES, lanes), 0) == coarse).astype(jnp.float32)
 
 
-def kernel(counts, b_hbm, d_hbm, tab_ref, out_ref, *refs):
+def kernel(counts, b_hbm, d_hbm, tab_hbm, out_ref, *refs):
     NX, NY, NZ = counts
     NXP = max(8, NX)
     it = iter(refs)
-    eb, ed, e1, e2, e3, u2, u3, x3 = (next(it) for _ in range(8))
-    zs = [next(it) for _ in range(7)]
-    zr = [next(it) for _ in range(7)]
-    bx = [next(it) for _ in range(4)]
-    wx = [next(it) for _ in range(4)]
-    vx = [next(it) for _ in range(4)]
+    eb, ed, e1, e3, u2, u3, tab_ref = (next(it) for _ in range(7))
+    zs = [next(it) for _ in range(4)]
+    zr = [next(it) for _ in range(4)]
+    bx = [next(it) for _ in range(3)]
+    wx = [next(it) for _ in range(3)]
+    vx = [next(it) for _ in range(3)]
     pair, fine0 = next(it), next(it)
     row0, row1, row2, g1, g2, g3 = (next(it) for _ in range(6))
     tally = next(it)
@@ -94,7 +95,7 @@
             for name, count, step in zip(("gx", "gy", "gz"), counts, offset)
         )
 
-    for ref in (eb, ed, e1, e2, e3, u2, u3, x3, pair, *zs, *zr):
+    for ref in (eb, ed, e1, e3, u2, u3, pair, *zs, *zr):
         ref[...] = jnp.zeros(ref.shape, jnp.float32)
     n = SIZE[0]
     loads = []
@@ -104,6 +105,8 @@
         )
         load.start()
         loads.append(load)
+    table_load = pltpu.make_async_copy(tab_hbm, tab_ref, in_sem.at[2])
+    table_load.start()
 
     peers = set()
     for o in OFFSETS:
@@ -117,13 +120,13 @@
         pl.semaphore_signal(barrier, inc=1, device_id=device(o), device_id_type=MESH)
 
     lane = iota((1, LANES), 1)
-    low = jnp.bitwise_and(lane, 63)
-    halve = (
-        iota((LANES, LANES), 0) // 2 == iota((LANES, LANES), 1)
-    ).astype(jnp.float32) * 0.5
-
-    def coarsen_own(level, values, first):
-        half = SIZE[level] // 2
+    source_lane = iota((LANES, LANES), 0)
+    whole = (source_lane // 2 == iota((LANES, LANES), 1)).astype(jnp.float32) * 0.5
+    turned = source_lane // 2 + jnp.where(source_lane < 96, 0, 64)
+    turned = (turned == iota((LANES, LANES), 1)).astype(jnp.float32) * 0.5
+
+    def coarsen(values, first, halve):
+        half = values.shape[0] // 2
         rows = values.shape[1]
         pair[0:half, 0:rows, :] = pair_planes(values)
         top = pair[0:half, pl.ds(first, 8, stride=2), :]
@@ -131,17 +134,18 @@
         return lanes_dot(top, halve)
 
     def pack(level, which, fields):
-        r, bz = HALO[level], DEPTH[level]
+        r, bz, pitch = HALO[level], DEPTH[level], PITCH[level]
         joined = len(fields) == 1
+        low = jnp.bitwise_and(lane, pitch - 1)
         for side in range(2):
             start = bz - r if side else 0
             acc = jnp.zeros((SIZE[level], LANES), jnp.float32)
             for x in range(SIZE[level]):
                 for f, values in enumerate(fields):
-                    place = f * 64 + x * r
+                    place = f * pitch + x * r
                     shift = (place - start) % LANES
                     moved = values[x] if shift == 0 else pltpu.roll(values[x], shift, 1)
-                    seat = low if joined else lane - f * 64
+                    seat = low if joined else lane - f * pitch
                     acc = jnp.where((seat >= x * r) & (seat < x * r + r), moved, acc)
             zs[which][side, :, :] = acc
 
@@ -150,7 +154,7 @@
         planes = []
         for p in range(PLANES[level]):
             block, x = divmod(p - r + n, n)
-            seat = f * 64 + x * r
+            seat = f * PITCH[level] + x * r
             down = (LANES - r - seat) % LANES
             up = (bz - seat) % LANES
             below, above = zr[which][0, block], zr[which][1, block]
@@ -216,11 +220,11 @@
     def finish(pending):
         drain(recv_sem.at[pending[0]], pending[1])
 
-    def domain(level):
-        n, r, row, bz = SIZE[level], HALO[level], ROW[level], DEPTH[level]
+    def domain(level, r, row, rows):
+        n, bz = SIZE[level], DEPTH[level]
         lanes = 256 if level == 0 else LANES
-        px = iota((PLANES[level], 1, 1), 0) - r
-        py = iota((1, ROWS[level], 1), 1) - row
+        px = iota((n + 2 * r, 1, 1), 0) - r
+        py = iota((1, rows, 1), 1) - row
         pz = iota((1, 1, lanes), 2)
         pz = jnp.where(pz < bz + 32, pz, pz - lanes)
         ok = None
@@ -230,18 +234,18 @@
             ok = good if ok is None else ok & good
         return ok
 
-    def presmooth(level, b, d):
-        n, r = SIZE[level], HALO[level]
+    def extended(level):
+        return domain(level, HALO[level], ROW[level], ROWS[level])
+
+    def presmooth(b, d, inside, extra, r):
+        n = b.shape[0] - 2 * r
         diag = 6.0 + d
-        w = jnp.where(domain(level), RELAX / diag, 0.0)
-        bx[level][...] = b
-        wx[level][...] = w
-        v = w * b
-        v = sweep(v, b[1:-1], w[1:-1])
-        vx[level][...] = v
-        near = v[r - 2 : r + n]
-        own = near[1:-1]
-        return (b[r : r + n] - diag[r : r + n] * own + neighbour_sum(near))[:, :, :LANES]
+        w = jnp.where(inside, RELAX / diag, 0.0)
+        v = sweep(w * b, b[1:-1], w[1:-1])
+        near = v[r - extra - 2 : r + n + extra]
+        mid = slice(r - extra, r + n + extra)
+        rest = b[mid] - diag[mid] * near[1:-1] + neighbour_sum(near)
+        return w, v, rest[:, :, :LANES]
 
     own_damping = []
     for load in loads:
@@ -253,7 +257,7 @@
 
     values = d_own
     for level in range(LEVELS - 1):
-        coarse = coarsen_own(level, values, 0)
+        coarse = coarsen(values, 0, whole)
         own_damping.append(coarse)
         values = coarse
     d_last = own_damping[-1]
@@ -270,108 +274,172 @@
     finish(copies)
     b0 = jnp.concatenate([eb[...], unpack(0, 0, 0)], axis=2)
     d0 = jnp.concatenate([ed[...], unpack(0, 0, 1)], axis=2)
-    remainder = presmooth(0, b0, d0)
-
-    hidden = None
-    for level, block in ((1, e1), (2, e2), (3, e3)):
-        n, r, row, bz = SIZE[level], HALO[level], ROW[level], DEPTH[level]
-        coarse = coarsen_own(level - 1, remainder, ROW[level - 1])
-        both = jnp.where(lane < 64, coarse, pltpu.roll(own_damping[level - 1], 64, 2))
-        both = both[:, :n]
-        block[pl.ds(r, n), pl.ds(row, n), :] = both
-        pack(level, level, (both,))
-        copies = exchange(level, level, (block,), (0, 1, 2, 1)[level])
-        finish(copies)
+    bx[0][...] = b0
+    wx[0][...], vx[0][...], remainder = presmooth(b0, d0, extended(0), 0, HALO[0])
+
+    def joined_rows(level, fields):
+        out = fields[0]
+        for k, values in enumerate(fields[1:], 1):
+            out = jnp.where(lane < k * PITCH[level], out, pltpu.roll(values, k * PITCH[level], 2))
+        return out
+
+    def send(level, which, block, values, turn_set):
+        n, r, row = SIZE[level], HALO[level], ROW[level]
+        block[pl.ds(r, n), pl.ds(row, n), :] = values
+        pack(level, which, (values,))
+        return exchange(level, which, (block,), turn_set)
+
+    def received(level, which, block, count):
         e = block[...]
-        b = jnp.where(lane < bz, e, unpack(level, level, 0))
-        d = jnp.where(lane < bz, pltpu.roll(e, 64, 2), unpack(level, level, 1))
-        remainder = presmooth(level, b, d)
-        if level >= 2:
-            own = vx[level][pl.ds(r - 1, n), pl.ds(row, n), :]
-            which = level + 2
-            target = (u2, u3)[level - 2]
-            target[pl.ds(r, n), pl.ds(row, n), :] = own
-            pack(level, which, (own,))
-            if hidden is not None:
-                finish(hidden)
-            hidden = exchange(level, which, (target,), (0, 2)[level - 2])
-
-    source = block_mean(
-        remainder,
-        (iota((8, LANES), 0) >= ROW[3])
-        & (iota((8, LANES), 0) < ROW[3] + SIZE[3])
-        & (iota((8, LANES), 1) < DEPTH[3]),
-    )
+        fields = []
+        for f in range(count):
+            own = pltpu.roll(e, LANES - f * PITCH[level], 2) if f else e
+            fields.append(jnp.where(lane < DEPTH[level], own, unpack(level, which, f)))
+        return fields
+
+    coarse = coarsen(remainder, ROW[0], whole)
+    finish(send(1, 1, e1, joined_rows(1, (coarse, own_damping[0]))[:, : SIZE[1]], 1))
+    b, d = received(1, 1, e1, 2)
+    bx[1][...] = b
+    wx[1][...], vx[1][...], remainder = presmooth(b, d, extended(1), 4, HALO[1])
+    b = coarsen(remainder, ROW[1] - 4, turned)
+    d = coarsen(d[HALO[1] - 4 : HALO[1] + SIZE[1] + 4], ROW[1] - 4, turned)
+    _, v, remainder = presmooth(b, d, domain(2, 2, 2, 8), 0, 2)
+    n = SIZE[2]
+    own = joined_rows(2, (b[2 : 2 + n], d[2 : 2 + n], v[1 : 1 + n]))
+    own = own[:, 2 : 2 + n]
+    coarse = coarsen(remainder, 2, whole)
+
+    d3 = coarsen(d, 0, turned)
+    at_row, at_lane = iota((1, 8, LANES), 1), iota((1, 8, LANES), 2)
+    near_lane = (at_lane <= DEPTH[3]) | (at_lane == LANES - 1)
+    none = jnp.zeros((1, 8, LANES), jnp.float32)
+    d3 = jnp.where((at_row >= 1) & (at_row <= 4) & near_lane, pltpu.roll(d3, 1, 1), 0.0)
+    d3 = jnp.concatenate([none, d3, none], axis=0)
+    mine = (at_row >= 2) & (at_row < 2 + SIZE[3]) & (at_lane < DEPTH[3])
+    b3 = jnp.where(mine, pltpu.roll(coarse, 2, 1), 0.0)
+    b3 = jnp.concatenate([none, none, b3, none, none], axis=0)
+    diag = 6.0 + d3
+    w3 = jnp.where(domain(3, 2, 2, 8), RELAX / diag, 0.0)
+    v = sweep(w3 * b3, b3[1:-1], w3[1:-1])
+    near = jnp.concatenate([none, none, v, none, none], axis=0)
+    parts = pair_planes(b3 - diag * near[1:-1] + neighbour_sum(near))
+    to = iota((LANES, LANES), 1)
+    side = jnp.where(source_lane < DEPTH[3], 0, jnp.where(source_lane < 64, 1, -1))
+    seat = (to % NZ == gz + side) & (to < 3 * NZ)
+    seat = seat & ((source_lane < DEPTH[3] + 2) | (source_lane >= LANES - 2))
+    parts = lanes_dot(parts, seat.astype(jnp.float32)) * last_scale
+    parts = jnp.where((at_row < 6) & (at_row // 2 == at_lane // NZ), parts, 0.0)
+    parts = jnp.sum(parts, axis=1, keepdims=True)
+
+    def rows_of(values):
+        row = iota((8, LANES), 0)
+        out = jnp.where(row == 0, values[0], jnp.where(row == 1, values[1], values[2]))
+        return jnp.where(row < 3, out, 0.0)
 
     def send_line(axis, src, dst):
         here, count = (gx, gy, gz)[axis], counts[axis]
         for k in range(1, count):
             offset = tuple(k if a == axis else 0 for a in range(3))
             pltpu.make_async_remote_copy(
-                src_ref=src.at[pl.ds(0, 1)],
-                dst_ref=dst.at[pl.ds(here, 1)],
+                src_ref=src.at[pl.ds(0, 3)],
+                dst_ref=dst.at[here, pl.ds(0, 3)],
                 send_sem=line_send.at[axis],
                 recv_sem=line_recv.at[axis],
                 device_id=device(offset),
                 device_id_type=MESH,
             ).start()
 
-    def finish_line(axis):
-        drain(line_recv.at[axis], counts[axis] - 1)
-
     def line_rows(axis, own, dst):
+        drain(line_recv.at[axis], 3 * (counts[axis] - 1))
         here, count = (gx, gy, gz)[axis], counts[axis]
-        rows = iota(dst.shape, 0)
-        got = jnp.where(rows == here, own, dst[...])
-        return jnp.where(rows < count, got, 0.0), rows
-
-    own0 = jnp.where(lane < 64, source, damping_mean)
-    row0[...] = jnp.broadcast_to(own0, (8, LANES))
+        places = iota(dst.shape, 0)
+        got = jnp.where(places == here, own, dst[...])
+        return jnp.where((places < count) & (iota(dst.shape, 1) < 3), got, 0.0)
+
+    own0 = jnp.where(lane < 64, rows_of(parts), damping_mean)
+    row0[...] = own0
     send_line(2, row0, g1)
-    finish_line(2)
-    got, rows = line_rows(2, own0, g1)
-    own1 = jnp.sum(
-        jnp.where((lane >= 64) | (lane % NZ == rows), got, 0.0), axis=0, keepdims=True
+    copies = send(3, 3, e3, joined_rows(3, (coarse, own_damping[2]))[:, : SIZE[3]], 2)
+    hidden = send(2, 2, u2, own, 3)
+
+    got = jnp.sum(line_rows(2, own0, g1), axis=0)
+    at_y = lane // NZ + (gy - 1)
+    moved = jnp.where((lane < 3 * NZ) & (at_y >= 0) & (at_y < NY), got, 0.0)
+    moved = pltpu.roll(moved, lax.rem((gy - 1) * NZ + LANES, LANES), 1)
+    own1 = jnp.where(lane < 64, moved, got)
+    row1[...] = own1
+    send_line(1, row1, g2)
+
+    def relay(turn_set, moves):
+        rows = 0
+        for o, first, size, target in moves:
+            rows += math.prod(size)
+            pltpu.make_async_remote_copy(
+                src_ref=u3.at[tuple(pl.ds(f, c) for f, c in zip(first, size))],
+                dst_ref=u3.at[tuple(pl.ds(f, c) for f, c in zip(target, size))],
+                send_sem=send_sem.at[turn_set],
+                recv_sem=recv_sem.at[turn_set],
+                device_id=device(o),
+                device_id_type=MESH,
+            ).start()
+        unsent[turn_set] = rows
+        return turn_set, rows
+
+    finish(copies)
+    b, d = received(3, 3, e3, 2)
+    _, v, _ = presmooth(b, d, extended(3), 0, HALO[3])
+    n, row = SIZE[3], ROW[3]
+    block3 = jnp.where(lane < 32, b, jnp.where(lane < 64, pltpu.roll(d, 32, 2), 0.0))[2 : 2 + n]
+    block3 = jnp.where(lane < 64, block3, pltpu.roll(v[1 : 1 + n], 64, 2))
+    u3[1, pl.ds(4, n), pl.ds(4, n), :] = block3[:, row : row + n]
+    steps = (-2, -1, 1, 2)
+    copies = relay(4, [((0, 0, o), (1, 4, 4), (1, n, n), (1 - o, 4, 4)) for o in (-1, 1)])
+    got = jnp.sum(line_rows(1, own1, g2), axis=0)
+    own2 = got
+    row2[...] = own2
+    send_line(0, row2, g3)
+    finish(copies)
+    copies = relay(
+        5, [((o, 0, 0), (0, 4, 4), (3, n, n), (0, 4 - n * o, 4)) for o in steps]
     )
-    row1[...] = jnp.broadcast_to(own1, (8, LANES))
-    send_line(1, row1, g2)
-    finish_line(1)
-    got, rows = line_rows(1, own1, g2)
-    own2 = jnp.sum(
-        jnp.where((lane >= 64) | (lane // NZ == rows), got, 0.0), axis=0, keepdims=True
+    finish(hidden)
+    b, d, smooth2 = received(2, 2, u2, 3)
+    bx[2][...] = b
+    wx[2][...] = jnp.where(extended(2), RELAX / (6.0 + d), 0.0)
+    vx[2][...] = jnp.where(extended(2), smooth2, 0.0)
+    finish(copies)
+    copies = relay(
+        6, [((0, o, 0), (0, 0, 4), (3, 8 + n, n), (0, 0, 4 - n * o)) for o in steps]
     )
-    row2[...] = jnp.broadcast_to(own2, (8, LANES))
-    send_line(0, row2, g3)
-    finish(hidden)
-    finish_line(0)
-    got, rows = line_rows(0, own2, g3)
-    mean = jnp.sum(got, axis=0, keepdims=True) * (1.0 / (NX * NY * NZ))
-    mean = jnp.where(lane < 64, pltpu.roll(mean, 64, 1), 0.0)
+    table_load.wait()
+    dot = functools.partial(jnp.dot, precision=HI, preferred_element_type=jnp.float32)
     table_x = tab_ref[0:NXP, 0:NXP]
     table_yz = tab_ref[pl.ds(16, LANES), :]
     eigen = tab_ref[pl.ds(16 + LANES, NXP), :]
-    dot = functools.partial(jnp.dot, precision=HI, preferred_element_type=jnp.float32)
-    spectrum = dot(dot(table_x, jnp.where(lane < NY * NZ, got, 0.0)), table_yz)
+    from_row = iota((NXP, 8 * NXP), 1)
+    sums = (from_row // 8 + from_row % 8 - 1 == iota((NXP, 8 * NXP), 0)) & (from_row % 8 < 3)
+    table_sum = dot(table_x, sums.astype(jnp.float32))
+    got = line_rows(0, own2, g3)
+    mean = jnp.sum(got, axis=0)[0:1] * (1.0 / (NX * NY * NZ))
+    mean = jnp.where(lane < 64, pltpu.roll(mean, 64, 1), 0.0)
+    got = jnp.where(lane < NY * NZ, got.reshape(8 * NXP, LANES), 0.0)
+    spectrum = dot(dot(table_sum, got), table_yz)
     spectrum = spectrum / (eigen + mean)
     coarse = dot(dot(table_x, spectrum), table_yz)
 
-    pick = iota((8, NXP), 1) == gx - 1 + iota((8, NXP), 0) // 2
+    pick = iota((16, NXP), 1) == gx - 2 + iota((16, NXP), 0) // 2
     along_x = dot(pick.astype(jnp.float32), coarse)
-    wanted = iota((8, LANES), 1) // NZ == gy - 1 + iota((8, LANES), 0) // 2
+    wanted = iota((16, LANES), 1) // NZ == gy - 2 + iota((16, LANES), 0) // 2
     spread = jnp.stack(
         [
-            jnp.where(wanted, jnp.broadcast_to(along_x[p : p + 1], (8, LANES)), 0.0)
-            for p in range(PLANES[3])
+            jnp.where(wanted, jnp.broadcast_to(along_x[p : p + 1], (16, LANES)), 0.0)
+            for p in range(8 + SIZE[3])
         ],
         axis=0,
     )
-    lane_to = iota((LANES, LANES), 1)
-    block_z = jnp.where(lane_to < DEPTH[3], 0, jnp.where(lane_to < 64, 1, -1))
-    seat = iota((LANES, LANES), 0) % NZ == gz + block_z
+    seat = source_lane % NZ == gz + jnp.where(to < DEPTH[3], 0, jnp.where(to < 64, 1, -1))
     correction = lanes_dot(spread, seat.astype(jnp.float32))
-
-    def halo_values(level, block, which):
-        return jnp.where(lane < DEPTH[level], block[...], unpack(level, which, 0))
 
     def postsmooth(level, v, start):
         for _ in range(2):
@@ -380,17 +448,21 @@
             v = sweep(v, bx[level][pl.ds(start, count)], wx[level][pl.ds(start, count)])
         return v
 
-    def in_domain(level, v):
-        return jnp.where(domain(level), v, 0.0)
-
-    v = in_domain(3, halo_values(3, u3, 5) + correction)
-    v = postsmooth(3, v, 0)
-    own = v[:, ROW[3] : ROW[3] + SIZE[3]]
-    x3[pl.ds(HALO[3], SIZE[3]), pl.ds(ROW[3], SIZE[3]), :] = own
-    pack(3, 6, (own,))
-    copies = exchange(3, 6, (x3,), 0)
     finish(copies)
-    v = in_domain(3, halo_values(3, x3, 6))
+    fields = []
+    for f in range(3):
+        here, below, above = (u3[k] for k in (1, 0, 2))
+        here = pltpu.roll(here, LANES - 32 * f, 2) if f == 1 or f == 2 else here
+        below = pltpu.roll(below, LANES - DEPTH[3] - 32 * f, 2)
+        above = pltpu.roll(above, (LANES + DEPTH[3] - 32 * f) % LANES, 2)
+        outer = jnp.where(lane < DEPTH[3] + 4, above, jnp.where(lane >= LANES - 4, below, 0.0))
+        fields.append(jnp.where(lane < DEPTH[3], here, outer))
+    b3, d3, smooth3 = fields
+    inside = domain(3, 4, 4, 16)
+    w3 = jnp.where(inside, RELAX / (6.0 + d3), 0.0)
+    v = jnp.where(inside, smooth3 + correction, 0.0)
+    v = sweep(v, b3[1:-1], w3[1:-1])
+    v = sweep(v, b3[2:-2], w3[2:-2])
 
     def refined(level, v, first):
         lanes = 256 if level == 0 else LANES
@@ -408,16 +480,16 @@
         full = jnp.broadcast_to(full[:, None], (planes, 2, ROWS[level], lanes))
         return full.reshape(2 * planes, ROWS[level], lanes)
 
-    v = halo_values(2, u2, 4) + refined(2, v, 0)
-    v = postsmooth(2, in_domain(2, v), 0)
-    correction = refined(1, v, ROW[2] - 2)
-    v = vx[1][...] + correction[1:-1]
-    v = postsmooth(1, v, 1)
-    correction = refined(0, v, ROW[1] - 2)
+    v = vx[2][...] + refined(2, v, 4 - ROW[2] // 2)
+    v = postsmooth(2, v, 0)
+    correction = refined(1, v, ROW[2] - ROW[1] // 2)
+    v = vx[1][pl.ds(2, 14)] + correction[1:-1]
+    v = postsmooth(1, v, 3)
+    correction = refined(0, v, ROW[1] - ROW[0] // 2)
     v = vx[0][...] + correction
     v = postsmooth(0, v, 1)
     for axis in range(3):
-        drain(line_send.at[axis], counts[axis] - 1)
+        drain(line_send.at[axis], 3 * (counts[axis] - 1))
     for turn_set in list(unsent):
         sent(turn_set)
     out_ref[...] = v[:, ROW[0] : ROW[0] + SIZE[0], :LANES]
@@ -451,30 +523,31 @@
 
     def local(divergence, damping):
         ext = [(p, r, LANES) for p, r in zip(PLANES, ROWS)]
-        levels = (0, 1, 2, 3, 2, 3, 3)
-        wide = [(p, r, 256 if k == 0 else LANES) for k, (p, r) in enumerate(zip(PLANES, ROWS))]
+        levels = (0, 1, 2, 3)
+        wide = [(p, r, 256 if k == 0 else LANES) for k, (p, r) in enumerate(zip(PLANES, ROWS))][:3]
         inner = [(p - 2, r, z) for p, r, z in wide]
-        shapes = [ext[0], ext[0], ext[1], ext[2], ext[3], ext[2], ext[3], ext[3]]
+        inner[2] = wide[2]
+        shapes = [ext[0], ext[0], ext[1], ext[3], ext[2], (3, 10, 16, LANES), (32 + LANES, LANES)]
         shapes += [(2, SIZE[k], LANES) for k in levels]
         shapes += [(2, 3, ROWS[k], LANES) for k in levels]
         shapes += wide + wide + inner
         shapes += [(8, 24, LANES), (12, 24, LANES)]
         shapes += [(8, LANES)] * 3
-        shapes += [(8, LANES), (8, LANES), (NXP, LANES), (2048, LANES)]
+        shapes += [(8, 8, LANES), (8, 8, LANES), (NXP, 8, LANES), (1024, LANES)]
         dma = pltpu.SemaphoreType.DMA
-        sems = [dma((3,)), dma((3,)), dma((3,)), dma((3,)), dma((2,))]
+        sems = [dma((7,)), dma((7,)), dma((3,)), dma((3,)), dma((3,))]
         return pl.pallas_call(
             functools.partial(kernel, counts),
             out_shape=jax.ShapeDtypeStruct(divergence.shape, f32),
             in_specs=[
-                pl.BlockSpec(memory_space=pl.ANY),
-                pl.BlockSpec(memory_space=pl.ANY),
-                pl.BlockSpec(memory_space=pltpu.VMEM),
+                pl.BlockSpec(memory_space=pltpu.HBM),
+                pl.BlockSpec(memory_space=pltpu.HBM),
+                pl.BlockSpec(memory_space=pltpu.HBM),
             ],
             out_specs=pl.BlockSpec(memory_space=pltpu.VMEM),
             scratch_shapes=[pltpu.VMEM(s, f32) for s in shapes] + sems,
             compiler_params=pltpu.CompilerParams(
-                collective_id=0, has_side_effects=True, vmem_limit_bytes=48 * 1024 * 1024
+                collective_id=0, has_side_effects=True
             ),
             name="vcycle",
         )(divergence, damping, jnp.asarray(tables(counts)))

time: 71.5 us -> 56.5 us (0.79)
  Pallas kernels: 67.9 us -> 54.3 us
  local copies, waits for them, and re-layouts: 3.35 us -> 1.57 us
    pallas_call x1, Pallas kernels: 67.9 us -> 54.3 us  [local(): pl.pallas_call(functools.partial(kernel, counts), out_shape=jax.ShapeDtyp...]
    unnamed x7 -> x1, local copies, waits for them, and re-layouts: 3.35 us -> 1.57 us
where the time goes in v2:
time: 56.5 us; the launch traced here: 55.8 us
  Pallas kernels  54.3 us (96%)
  local copies, waits for them, and re-layouts  1.57 us (3%)
    pallas_call x1, Pallas kernels, local(): pl.pallas_call(functools.partial(kernel, counts), out_shape=jax.ShapeDtyp...  54.3 us
    unnamed x1, local copies, waits for them, and re-layouts  1.57 us

profile of v2, /device:TPU:1, one launch (start us, length us, event | category | flops | bytes accessed | tf_op | source)
XLA Modules:
  0.0 55.8 jit_solution(4920691791576553861)
XLA Ops:
  0.0 54.3 %vcycle.1 = f32[16,16,128]{2,1,0:T(8,128)} custom-call(f32[16,16,128]{2,1,0:T(8,128)} %b_hbm.1, f32[16,16,128]{2,1,0:T(8,128)} %d_hbm.1, f32[160,128]{1,0:T(8,128)} %constant.2.clone.tab_hbm), custom_call_target="tpu_custom_call" | custom-call | tf_op jit(solution)/shard_map/vcycle/pallas_call | solution.py:539
  54.3 1.6 %copy.5 = f32[16,16,128]{2,1,0:T(8,128)} copy(f32[16,16,128]{2,1,0:T(8,128)} %vcycle.1) | data formatting | bytes 262144

commit v3 on v2

--- a/solution.py
+++ b/solution.py
@@ -22,9 +22,16 @@
 PLANES = tuple(n + 2 * r for n, r in zip(SIZE, HALO))
 ROWS = (24, 24, 16, 8)
 PITCH = (64, 64, 32, 64)
+DEEP = (3, 6, 4, 5)
 OFFSETS = [o for o in itertools.product((-1, 0, 1), repeat=3) if o != (0, 0, 0)]
 FLAT = [o for o in OFFSETS if o[2] == 0]
 TALL = [o for o in OFFSETS if o[2] != 0]
+FAR = [
+    (x, y, 0)
+    for x in range(-2, 3)
+    for y in range(-2, 3)
+    if (x, y) != (0, 0) and abs(x) + abs(y) < 4
+]
 
 
 def iota(shape, axis):
@@ -105,11 +112,11 @@
         )
         load.start()
         loads.append(load)
-    table_load = pltpu.make_async_copy(tab_hbm, tab_ref, in_sem.at[2])
+    table_load = pltpu.make_async_copy(tab_hbm.at[pl.ds(0, 32 + LANES)], tab_ref, in_sem.at[2])
     table_load.start()
 
     peers = set()
-    for o in OFFSETS:
+    for o in OFFSETS + FAR:
         peers.add(tuple(s % c for s, c in zip(o, counts)))
     for axis in range(3):
         for k in range(1, counts[axis]):
@@ -134,7 +141,7 @@
         return lanes_dot(top, halve)
 
     def pack(level, which, fields):
-        r, bz, pitch = HALO[level], DEPTH[level], PITCH[level]
+        r, bz, pitch = DEEP[level], DEPTH[level], PITCH[level]
         joined = len(fields) == 1
         low = jnp.bitwise_and(lane, pitch - 1)
         for side in range(2):
@@ -150,10 +157,10 @@
             zs[which][side, :, :] = acc
 
     def unpack(level, which, f):
-        n, r, bz = SIZE[level], HALO[level], DEPTH[level] % LANES
+        n, wide, bz, r = SIZE[level], HALO[level], DEPTH[level] % LANES, DEEP[level]
         planes = []
         for p in range(PLANES[level]):
-            block, x = divmod(p - r + n, n)
+            block, x = divmod(p - wide + n, n)
             seat = f * PITCH[level] + x * r
             down = (LANES - r - seat) % LANES
             up = (bz - seat) % LANES
@@ -220,7 +227,7 @@
     def finish(pending):
         drain(recv_sem.at[pending[0]], pending[1])
 
-    def domain(level, r, row, rows):
+    def domain(level, r, row, rows, deep):
         n, bz = SIZE[level], DEPTH[level]
         lanes = 256 if level == 0 else LANES
         px = iota((n + 2 * r, 1, 1), 0) - r
@@ -228,14 +235,18 @@
         pz = iota((1, 1, lanes), 2)
         pz = jnp.where(pz < bz + 32, pz, pz - lanes)
         ok = None
-        for p, here, count, size in ((px, gx, NX, n), (py, gy, NY, n), (pz, gz, NZ, bz)):
+        for p, here, count, size, halo in (
+            (px, gx, NX, n, r),
+            (py, gy, NY, n, r),
+            (pz, gz, NZ, bz, deep),
+        ):
             at = p + here * size
-            good = (p >= -r) & (p < size + r) & (at >= 0) & (at < count * size)
+            good = (p >= -halo) & (p < size + halo) & (at >= 0) & (at < count * size)
             ok = good if ok is None else ok & good
         return ok
 
     def extended(level):
-        return domain(level, HALO[level], ROW[level], ROWS[level])
+        return domain(level, HALO[level], ROW[level], ROWS[level], DEEP[level])
 
     def presmooth(b, d, inside, extra, r):
         n = b.shape[0] - 2 * r
@@ -304,7 +315,7 @@
     wx[1][...], vx[1][...], remainder = presmooth(b, d, extended(1), 4, HALO[1])
     b = coarsen(remainder, ROW[1] - 4, turned)
     d = coarsen(d[HALO[1] - 4 : HALO[1] + SIZE[1] + 4], ROW[1] - 4, turned)
-    _, v, remainder = presmooth(b, d, domain(2, 2, 2, 8), 0, 2)
+    _, v, remainder = presmooth(b, d, domain(2, 2, 2, 8, 2), 0, 2)
     n = SIZE[2]
     own = joined_rows(2, (b[2 : 2 + n], d[2 : 2 + n], v[1 : 1 + n]))
     own = own[:, 2 : 2 + n]
@@ -320,7 +331,7 @@
     b3 = jnp.where(mine, pltpu.roll(coarse, 2, 1), 0.0)
     b3 = jnp.concatenate([none, none, b3, none, none], axis=0)
     diag = 6.0 + d3
-    w3 = jnp.where(domain(3, 2, 2, 8), RELAX / diag, 0.0)
+    w3 = jnp.where(domain(3, 2, 2, 8, 2), RELAX / diag, 0.0)
     v = sweep(w3 * b3, b3[1:-1], w3[1:-1])
     near = jnp.concatenate([none, none, v, none, none], axis=0)
     parts = pair_planes(b3 - diag * near[1:-1] + neighbour_sum(near))
@@ -371,47 +382,38 @@
     row1[...] = own1
     send_line(1, row1, g2)
 
-    def relay(turn_set, moves):
-        rows = 0
-        for o, first, size, target in moves:
-            rows += math.prod(size)
-            pltpu.make_async_remote_copy(
-                src_ref=u3.at[tuple(pl.ds(f, c) for f, c in zip(first, size))],
-                dst_ref=u3.at[tuple(pl.ds(f, c) for f, c in zip(target, size))],
-                send_sem=send_sem.at[turn_set],
-                recv_sem=recv_sem.at[turn_set],
-                device_id=device(o),
-                device_id_type=MESH,
-            ).start()
-        unsent[turn_set] = rows
-        return turn_set, rows
-
     finish(copies)
     b, d = received(3, 3, e3, 2)
     _, v, _ = presmooth(b, d, extended(3), 0, HALO[3])
     n, row = SIZE[3], ROW[3]
-    block3 = jnp.where(lane < 32, b, jnp.where(lane < 64, pltpu.roll(d, 32, 2), 0.0))[2 : 2 + n]
-    block3 = jnp.where(lane < 64, block3, pltpu.roll(v[1 : 1 + n], 64, 2))
-    u3[1, pl.ds(4, n), pl.ds(4, n), :] = block3[:, row : row + n]
-    steps = (-2, -1, 1, 2)
-    copies = relay(4, [((0, 0, o), (1, 4, 4), (1, n, n), (1 - o, 4, 4)) for o in (-1, 1)])
-    got = jnp.sum(line_rows(1, own1, g2), axis=0)
-    own2 = got
+    block3 = None
+    for f, values in enumerate((b[2 : 2 + n], d[2 : 2 + n], v[1 : 1 + n])):
+        values = jnp.where(lane < 24, values, pltpu.roll(values, 32, 2))
+        if f:
+            block3 = jnp.where(lane < 32 * f, block3, pltpu.roll(values, 32 * f, 2))
+        else:
+            block3 = values
+    u3[pl.ds(4, n), pl.ds(4, n), :] = block3[:, row : row + n]
+    for o in FAR:
+        pltpu.make_async_remote_copy(
+            src_ref=u3.at[pl.ds(4, n), pl.ds(4, n)],
+            dst_ref=u3.at[pl.ds(4 - n * o[0], n), pl.ds(4 - n * o[1], n)],
+            send_sem=send_sem.at[4],
+            recv_sem=recv_sem.at[4],
+            device_id=device(o),
+            device_id_type=MESH,
+        ).start()
+    unsent[4] = len(FAR) * n * n
+    copies = (4, len(FAR) * n * n)
+
+    own2 = jnp.sum(line_rows(1, own1, g2), axis=0)
     row2[...] = own2
     send_line(0, row2, g3)
-    finish(copies)
-    copies = relay(
-        5, [((o, 0, 0), (0, 4, 4), (3, n, n), (0, 4 - n * o, 4)) for o in steps]
-    )
     finish(hidden)
     b, d, smooth2 = received(2, 2, u2, 3)
     bx[2][...] = b
     wx[2][...] = jnp.where(extended(2), RELAX / (6.0 + d), 0.0)
     vx[2][...] = jnp.where(extended(2), smooth2, 0.0)
-    finish(copies)
-    copies = relay(
-        6, [((0, o, 0), (0, 0, 4), (3, 8 + n, n), (0, 0, 4 - n * o)) for o in steps]
-    )
     table_load.wait()
     dot = functools.partial(jnp.dot, precision=HI, preferred_element_type=jnp.float32)
     table_x = tab_ref[0:NXP, 0:NXP]
@@ -420,16 +422,27 @@
     from_row = iota((NXP, 8 * NXP), 1)
     sums = (from_row // 8 + from_row % 8 - 1 == iota((NXP, 8 * NXP), 0)) & (from_row % 8 < 3)
     table_sum = dot(table_x, sums.astype(jnp.float32))
+    pick = iota((16, NXP), 1) == gx - 2 + iota((16, NXP), 0) // 2
+    table_pick = dot(pick.astype(jnp.float32), table_x)
+    finish(copies)
+    e = u3[...]
+    fields = []
+    for f in range(3):
+        values = pltpu.roll(e, LANES - 32 * f, 2) if f else e
+        outer = jnp.where(lane >= LANES - 4, pltpu.roll(values, 96, 2), 0.0)
+        fields.append(jnp.where(lane < DEPTH[3] + 4, values, outer))
+    b3, d3, smooth3 = fields
+    inside = domain(3, 4, 4, 16, 4)
+    w3 = jnp.where(inside, RELAX / (6.0 + d3), 0.0)
+
     got = line_rows(0, own2, g3)
     mean = jnp.sum(got, axis=0)[0:1] * (1.0 / (NX * NY * NZ))
     mean = jnp.where(lane < 64, pltpu.roll(mean, 64, 1), 0.0)
     got = jnp.where(lane < NY * NZ, got.reshape(8 * NXP, LANES), 0.0)
     spectrum = dot(dot(table_sum, got), table_yz)
     spectrum = spectrum / (eigen + mean)
-    coarse = dot(dot(table_x, spectrum), table_yz)
-
-    pick = iota((16, NXP), 1) == gx - 2 + iota((16, NXP), 0) // 2
-    along_x = dot(pick.astype(jnp.float32), coarse)
+    along_x = dot(dot(table_pick, spectrum), table_yz)
+
     wanted = iota((16, LANES), 1) // NZ == gy - 2 + iota((16, LANES), 0) // 2
     spread = jnp.stack(
         [
@@ -448,18 +461,6 @@
             v = sweep(v, bx[level][pl.ds(start, count)], wx[level][pl.ds(start, count)])
         return v
 
-    finish(copies)
-    fields = []
-    for f in range(3):
-        here, below, above = (u3[k] for k in (1, 0, 2))
-        here = pltpu.roll(here, LANES - 32 * f, 2) if f == 1 or f == 2 else here
-        below = pltpu.roll(below, LANES - DEPTH[3] - 32 * f, 2)
-        above = pltpu.roll(above, (LANES + DEPTH[3] - 32 * f) % LANES, 2)
-        outer = jnp.where(lane < DEPTH[3] + 4, above, jnp.where(lane >= LANES - 4, below, 0.0))
-        fields.append(jnp.where(lane < DEPTH[3], here, outer))
-    b3, d3, smooth3 = fields
-    inside = domain(3, 4, 4, 16)
-    w3 = jnp.where(inside, RELAX / (6.0 + d3), 0.0)
     v = jnp.where(inside, smooth3 + correction, 0.0)
     v = sweep(v, b3[1:-1], w3[1:-1])
     v = sweep(v, b3[2:-2], w3[2:-2])
@@ -507,11 +508,11 @@
         return (2.0 - 2.0 * np.cos(math.pi * index / (points + 1))) / (spacing * spacing)
 
     nx, ny, nz = counts
-    out = np.zeros((16 + LANES + 16, LANES))
+    out = np.zeros((1024, LANES))
     out[:nx, :nx] = sine(nx)
     out[16 : 16 + ny * nz, : ny * nz] = np.kron(sine(ny), sine(nz))
     plane = eigen(ny, 16.0)[:, None] + eigen(nz, 128.0)[None, :]
-    out[16 + LANES :] = 1.0
+    out[16 + LANES : 32 + LANES] = 1.0
     out[16 + LANES : 16 + LANES + nx, : ny * nz] = eigen(nx, 16.0)[:, None] + plane.reshape(1, -1)
     return out.astype(np.float32)
 
@@ -527,7 +528,7 @@
         wide = [(p, r, 256 if k == 0 else LANES) for k, (p, r) in enumerate(zip(PLANES, ROWS))][:3]
         inner = [(p - 2, r, z) for p, r, z in wide]
         inner[2] = wide[2]
-        shapes = [ext[0], ext[0], ext[1], ext[3], ext[2], (3, 10, 16, LANES), (32 + LANES, LANES)]
+        shapes = [ext[0], ext[0], ext[1], ext[3], ext[2], (10, 16, LANES), (32 + LANES, LANES)]
         shapes += [(2, SIZE[k], LANES) for k in levels]
         shapes += [(2, 3, ROWS[k], LANES) for k in levels]
         shapes += wide + wide + inner
@@ -535,7 +536,7 @@
         shapes += [(8, LANES)] * 3
         shapes += [(8, 8, LANES), (8, 8, LANES), (NXP, 8, LANES), (1024, LANES)]
         dma = pltpu.SemaphoreType.DMA
-        sems = [dma((7,)), dma((7,)), dma((3,)), dma((3,)), dma((3,))]
+        sems = [dma((5,)), dma((5,)), dma((3,)), dma((3,)), dma((3,))]
         return pl.pallas_call(
             functools.partial(kernel, counts),
             out_shape=jax.ShapeDtypeStruct(divergence.shape, f32),
@@ -547,7 +548,7 @@
             out_specs=pl.BlockSpec(memory_space=pltpu.VMEM),
             scratch_shapes=[pltpu.VMEM(s, f32) for s in shapes] + sems,
             compiler_params=pltpu.CompilerParams(
-                collective_id=0, has_side_effects=True
+                collective_id=0, has_side_effects=True, vmem_limit_bytes=55000 * 1024
             ),
             name="vcycle",
         )(divergence, damping, jnp.asarray(tables(counts)))

time: 56.5 us -> 54.2 us (0.959)
  local copies, waits for them, and re-layouts: 1.57 us -> 0.66 us
  Pallas kernels: 54.3 us -> 53.4 us
    unnamed x1, local copies, waits for them, and re-layouts: 1.57 us -> 0.66 us
    pallas_call x1, Pallas kernels: 54.3 us -> 53.4 us  [local(): pl.pallas_call(functools.partial(kernel, counts), out_shape=jax.ShapeDtyp...]
where the time goes in v3:
time: 54.2 us; the launch traced here: 54.1 us
  Pallas kernels  53.4 us (99%)
  local copies, waits for them, and re-layouts  0.66 us (1%)
    pallas_call x1, Pallas kernels, local(): pl.pallas_call(functools.partial(kernel, counts), out_shape=jax.ShapeDtyp...  53.4 us

profile of v3, /device:TPU:1, one launch (start us, length us, event | category | flops | bytes accessed | tf_op | source)
XLA Modules:
  0.0 54.1 jit_solution(15431243631730543980)
XLA Ops:
  0.0 53.4 %vcycle.1 = f32[16,16,128]{2,1,0:T(8,128)S(1)} custom-call(f32[16,16,128]{2,1,0:T(8,128)} %b_hbm.1, f32[16,16,128]{2,1,0:T(8,128)} %d_hbm.1, f32[1024,128]{1,0:T(8,128)} %constant.2.clone.tab_hbm), custom_call_target="tpu_custom_call" | custom-call | tf_op jit(solution)/shard_map/vcycle/pallas_call | solution.py:540
  53.4 0.7 %copy.5 = f32[16,16,128]{2,1,0:T(8,128)} copy(f32[16,16,128]{2,1,0:T(8,128)S(1)} %vcycle.1) | data formatting | bytes 262144

commit v4 on v3

--- a/solution.py
+++ b/solution.py
@@ -58,9 +58,14 @@
 
 def lanes_dot(v, table):
     planes, rows, lanes = v.shape
-    out = jnp.dot(
-        v.reshape(planes * rows, lanes), table, precision=HI, preferred_element_type=jnp.float32
-    )
+    flat = v.reshape(planes * rows, lanes)
+    parts = []
+    for _ in range(3):
+        parts.append(flat.astype(jnp.bfloat16))
+        flat = flat - parts[-1].astype(jnp.float32)
+    table = table.astype(jnp.bfloat16)
+    dot = functools.partial(jnp.dot, preferred_element_type=jnp.float32)
+    out = dot(parts[0], table) + (dot(parts[1], table) + dot(parts[2], table))
     return out.reshape(planes, rows, table.shape[1])
 
 
@@ -76,14 +81,14 @@
     NX, NY, NZ = counts
     NXP = max(8, NX)
     it = iter(refs)
-    eb, ed, e1, e3, u2, u3, tab_ref = (next(it) for _ in range(7))
+    e0, e1, e3, u2, u3, tab_ref = (next(it) for _ in range(6))
     zs = [next(it) for _ in range(4)]
     zr = [next(it) for _ in range(4)]
     bx = [next(it) for _ in range(3)]
     wx = [next(it) for _ in range(3)]
     vx = [next(it) for _ in range(3)]
     pair, fine0 = next(it), next(it)
-    row0, row1, row2, g1, g2, g3 = (next(it) for _ in range(6))
+    row1, row2, g1, g3 = (next(it) for _ in range(4))
     tally = next(it)
     send_sem, recv_sem, line_send, line_recv, in_sem = (next(it) for _ in range(5))
 
@@ -102,13 +107,13 @@
             for name, count, step in zip(("gx", "gy", "gz"), counts, offset)
         )
 
-    for ref in (eb, ed, e1, e3, u2, u3, pair, *zs, *zr):
+    for ref in (e0, e1, e3, u2, u3, pair, *zs, *zr):
         ref[...] = jnp.zeros(ref.shape, jnp.float32)
     n = SIZE[0]
     loads = []
-    for k, (src, dst) in enumerate(((b_hbm, eb), (d_hbm, ed))):
+    for k, src in enumerate((b_hbm, d_hbm)):
         load = pltpu.make_async_copy(
-            src, dst.at[pl.ds(HALO[0], n), pl.ds(ROW[0], n)], in_sem.at[k]
+            src, e0.at[k, pl.ds(HALO[0], n), pl.ds(ROW[0], n)], in_sem.at[k]
         )
         load.start()
         loads.append(load)
@@ -118,12 +123,15 @@
     peers = set()
     for o in OFFSETS + FAR:
         peers.add(tuple(s % c for s, c in zip(o, counts)))
-    for axis in range(3):
-        for k in range(1, counts[axis]):
-            peers.add(tuple(k if a == axis else 0 for a in range(3)))
+    line = [(k, 0, 0) for k in range(NX)]
+    plane = [(0, j, k) for j in range(NY) for k in range(NZ)]
+    peers.update(line, plane)
     peers.discard((0, 0, 0))
     barrier = pltpu.get_barrier_semaphore()
-    for o in sorted(peers):
+    def steps(o):
+        return sum(min(s, c - s) for s, c in zip(o, counts))
+
+    for o in sorted(peers, key=lambda o: (steps(o), o)):
         pl.semaphore_signal(barrier, inc=1, device_id=device(o), device_id_type=MESH)
 
     lane = iota((1, LANES), 1)
@@ -183,7 +191,7 @@
         if turn_set in unsent:
             drain(send_sem.at[turn_set], unsent.pop(turn_set))
 
-    def exchange(level, which, blocks, turn_set):
+    def exchange(level, which, block, turn_set):
         n, r, row = SIZE[level], HALO[level], ROW[level]
         sent(turn_set)
         sems = dict(send_sem=send_sem.at[turn_set], recv_sem=recv_sem.at[turn_set])
@@ -206,19 +214,19 @@
         for o in FLAT:
             sx, cx = span(o[0], n, r)
             sy, cy = span(o[1], n, r)
-            for block in blocks:
-                rows += cx * cy
-                copies.append(
-                    pltpu.make_async_remote_copy(
-                        src_ref=block.at[pl.ds(r + sx, cx), pl.ds(row + sy, cy)],
-                        dst_ref=block.at[
-                            pl.ds(r + sx - o[0] * n, cx), pl.ds(row + sy - o[1] * n, cy)
-                        ],
-                        device_id=device(o),
-                        device_id_type=MESH,
-                        **sems,
-                    )
+            fields = (pl.ds(0, 2),) if level == 0 else ()
+            rows += cx * cy * (1 + len(fields))
+            copies.append(
+                pltpu.make_async_remote_copy(
+                    src_ref=block.at[fields + (pl.ds(r + sx, cx), pl.ds(row + sy, cy))],
+                    dst_ref=block.at[
+                        fields + (pl.ds(r + sx - o[0] * n, cx), pl.ds(row + sy - o[1] * n, cy))
+                    ],
+                    device_id=device(o),
+                    device_id_type=MESH,
+                    **sems,
                 )
+            )
         for copy in copies:
             copy.start()
         unsent[turn_set] = rows
@@ -261,10 +269,10 @@
     own_damping = []
     for load in loads:
         load.wait()
-    d_own = ed[pl.ds(HALO[0], n), pl.ds(ROW[0], n), :]
-    pack(0, 0, (eb[pl.ds(HALO[0], n), pl.ds(ROW[0], n), :], d_own))
+    d_own = e0[1, pl.ds(HALO[0], n), pl.ds(ROW[0], n), :]
+    pack(0, 0, (e0[0, pl.ds(HALO[0], n), pl.ds(ROW[0], n), :], d_own))
     pl.semaphore_wait(barrier, len(peers))
-    copies = exchange(0, 0, (eb, ed), 0)
+    copies = exchange(0, 0, e0, 0)
 
     values = d_own
     for level in range(LEVELS - 1):
@@ -283,8 +291,8 @@
     damping_mean = block_mean(d_last, own_nodes)
 
     finish(copies)
-    b0 = jnp.concatenate([eb[...], unpack(0, 0, 0)], axis=2)
-    d0 = jnp.concatenate([ed[...], unpack(0, 0, 1)], axis=2)
+    b0 = jnp.concatenate([e0[0], unpack(0, 0, 0)], axis=2)
+    d0 = jnp.concatenate([e0[1], unpack(0, 0, 1)], axis=2)
     bx[0][...] = b0
     wx[0][...], vx[0][...], remainder = presmooth(b0, d0, extended(0), 0, HALO[0])
 
@@ -298,7 +306,7 @@
         n, r, row = SIZE[level], HALO[level], ROW[level]
         block[pl.ds(r, n), pl.ds(row, n), :] = values
         pack(level, which, (values,))
-        return exchange(level, which, (block,), turn_set)
+        return exchange(level, which, block, turn_set)
 
     def received(level, which, block, count):
         e = block[...]
@@ -348,39 +356,34 @@
         out = jnp.where(row == 0, values[0], jnp.where(row == 1, values[1], values[2]))
         return jnp.where(row < 3, out, 0.0)
 
-    def send_line(axis, src, dst):
-        here, count = (gx, gy, gz)[axis], counts[axis]
-        for k in range(1, count):
-            offset = tuple(k if a == axis else 0 for a in range(3))
+    def send_sums(stage, src, dst, here, offsets):
+        offsets = [o for o in offsets if o != (0, 0, 0)]
+        for o in sorted(offsets, key=steps, reverse=True):
             pltpu.make_async_remote_copy(
                 src_ref=src.at[pl.ds(0, 3)],
                 dst_ref=dst.at[here, pl.ds(0, 3)],
-                send_sem=line_send.at[axis],
-                recv_sem=line_recv.at[axis],
-                device_id=device(offset),
+                send_sem=line_send.at[stage],
+                recv_sem=line_recv.at[stage],
+                device_id=device(o),
                 device_id_type=MESH,
             ).start()
 
-    def line_rows(axis, own, dst):
-        drain(line_recv.at[axis], 3 * (counts[axis] - 1))
-        here, count = (gx, gy, gz)[axis], counts[axis]
+    def sums(stage, own, dst, here, count):
+        drain(line_recv.at[stage], 3 * (count - 1))
         places = iota(dst.shape, 0)
         got = jnp.where(places == here, own, dst[...])
         return jnp.where((places < count) & (iota(dst.shape, 1) < 3), got, 0.0)
 
-    own0 = jnp.where(lane < 64, rows_of(parts), damping_mean)
-    row0[...] = own0
-    send_line(2, row0, g1)
+    moved = rows_of(parts)
+    at_y = lane // NZ + (gy - 1)
+    moved = jnp.where((lane < 3 * NZ) & (at_y >= 0) & (at_y < NY), moved, 0.0)
+    moved = pltpu.roll(moved, lax.rem((gy - 1) * NZ + LANES, LANES), 1)
+    own1 = jnp.where(lane < 64, moved, damping_mean)
+    row1[...] = own1
+    here1 = gy * NZ + gz
+    send_sums(0, row1, g1, here1, plane)
     copies = send(3, 3, e3, joined_rows(3, (coarse, own_damping[2]))[:, : SIZE[3]], 2)
     hidden = send(2, 2, u2, own, 3)
-
-    got = jnp.sum(line_rows(2, own0, g1), axis=0)
-    at_y = lane // NZ + (gy - 1)
-    moved = jnp.where((lane < 3 * NZ) & (at_y >= 0) & (at_y < NY), got, 0.0)
-    moved = pltpu.roll(moved, lax.rem((gy - 1) * NZ + LANES, LANES), 1)
-    own1 = jnp.where(lane < 64, moved, got)
-    row1[...] = own1
-    send_line(1, row1, g2)
 
     finish(copies)
     b, d = received(3, 3, e3, 2)
@@ -406,9 +409,9 @@
     unsent[4] = len(FAR) * n * n
     copies = (4, len(FAR) * n * n)
 
-    own2 = jnp.sum(line_rows(1, own1, g2), axis=0)
+    own2 = jnp.sum(sums(0, own1, g1, here1, NY * NZ), axis=0)
     row2[...] = own2
-    send_line(0, row2, g3)
+    send_sums(1, row2, g3, gx, line)
     finish(hidden)
     b, d, smooth2 = received(2, 2, u2, 3)
     bx[2][...] = b
@@ -420,8 +423,8 @@
     table_yz = tab_ref[pl.ds(16, LANES), :]
     eigen = tab_ref[pl.ds(16 + LANES, NXP), :]
     from_row = iota((NXP, 8 * NXP), 1)
-    sums = (from_row // 8 + from_row % 8 - 1 == iota((NXP, 8 * NXP), 0)) & (from_row % 8 < 3)
-    table_sum = dot(table_x, sums.astype(jnp.float32))
+    picks = (from_row // 8 + from_row % 8 - 1 == iota((NXP, 8 * NXP), 0)) & (from_row % 8 < 3)
+    table_sum = dot(table_x, picks.astype(jnp.float32))
     pick = iota((16, NXP), 1) == gx - 2 + iota((16, NXP), 0) // 2
     table_pick = dot(pick.astype(jnp.float32), table_x)
     finish(copies)
@@ -435,7 +438,7 @@
     inside = domain(3, 4, 4, 16, 4)
     w3 = jnp.where(inside, RELAX / (6.0 + d3), 0.0)
 
-    got = line_rows(0, own2, g3)
+    got = sums(1, own2, g3, gx, NX)
     mean = jnp.sum(got, axis=0)[0:1] * (1.0 / (NX * NY * NZ))
     mean = jnp.where(lane < 64, pltpu.roll(mean, 64, 1), 0.0)
     got = jnp.where(lane < NY * NZ, got.reshape(8 * NXP, LANES), 0.0)
@@ -489,8 +492,8 @@
     correction = refined(0, v, ROW[1] - ROW[0] // 2)
     v = vx[0][...] + correction
     v = postsmooth(0, v, 1)
-    for axis in range(3):
-        drain(line_send.at[axis], 3 * (counts[axis] - 1))
+    drain(line_send.at[0], 3 * (NY * NZ - 1))
+    drain(line_send.at[1], 3 * (NX - 1))
     for turn_set in list(unsent):
         sent(turn_set)
     out_ref[...] = v[:, ROW[0] : ROW[0] + SIZE[0], :LANES]
@@ -528,15 +531,15 @@
         wide = [(p, r, 256 if k == 0 else LANES) for k, (p, r) in enumerate(zip(PLANES, ROWS))][:3]
         inner = [(p - 2, r, z) for p, r, z in wide]
         inner[2] = wide[2]
-        shapes = [ext[0], ext[0], ext[1], ext[3], ext[2], (10, 16, LANES), (32 + LANES, LANES)]
+        shapes = [(2, *ext[0]), ext[1], ext[3], ext[2], (10, 16, LANES), (32 + LANES, LANES)]
         shapes += [(2, SIZE[k], LANES) for k in levels]
         shapes += [(2, 3, ROWS[k], LANES) for k in levels]
         shapes += wide + wide + inner
         shapes += [(8, 24, LANES), (12, 24, LANES)]
-        shapes += [(8, LANES)] * 3
-        shapes += [(8, 8, LANES), (8, 8, LANES), (NXP, 8, LANES), (1024, LANES)]
+        shapes += [(8, LANES)] * 2
+        shapes += [(64, 8, LANES), (NXP, 8, LANES), (1024, LANES)]
         dma = pltpu.SemaphoreType.DMA
-        sems = [dma((5,)), dma((5,)), dma((3,)), dma((3,)), dma((3,))]
+        sems = [dma((5,)), dma((5,)), dma((2,)), dma((2,)), dma((3,))]
         return pl.pallas_call(
             functools.partial(kernel, counts),
             out_shape=jax.ShapeDtypeStruct(divergence.shape, f32),

time: 54.2 us -> 53.7 us (level)
  no operation moved by 1% of the time
where the time goes in v4:
time: 53.7 us; the launch traced here: 53.6 us
  Pallas kernels  52.9 us (99%)
  local copies, waits for them, and re-layouts  0.66 us (1%)
    pallas_call x1, Pallas kernels, local(): pl.pallas_call(functools.partial(kernel, counts), out_shape=jax.ShapeDtyp...  52.9 us

profile of v4, /device:TPU:1, one launch (start us, length us, event | category | flops | bytes accessed | tf_op | source)
XLA Modules:
  0.0 53.6 jit_solution(12310987014715576178)
XLA Ops:
  0.0 52.9 %vcycle.1 = f32[16,16,128]{2,1,0:T(8,128)S(1)} custom-call(f32[16,16,128]{2,1,0:T(8,128)} %b_hbm.1, f32[16,16,128]{2,1,0:T(8,128)} %d_hbm.1, f32[1024,128]{1,0:T(8,128)} %constant.2.clone.tab_hbm), custom_call_target="tpu_custom_call" | custom-call | tf_op jit(solution)/shard_map/vcycle/pallas_call | solution.py:543
  52.9 0.7 %copy.5 = f32[16,16,128]{2,1,0:T(8,128)} copy(f32[16,16,128]{2,1,0:T(8,128)S(1)} %vcycle.1) | data formatting | bytes 262144
